TPU v7x, 256 devices: a whole 4x4x8 slice. The times are simulated.
256 devices in a mesh: gx: 4 (over x), gy: 8 (over z_lo, core), gz: 8 (over y, z_hi).
Axes of the slice: x: 4, y: 4, z: 8 (z_hi: 2, z_lo: 4; z = z_hi * 4 + z_lo), core: 2. Of those that a mesh axis runs over, the one named last changes fastest.
Arguments:
- energy: float32 [256, 256, 1024], P(('gz', 'gy', 'gx')), may hold values from -5 to 5
- flow: float32 [4, 256, 256, 1024], P(None, ('gz', 'gy', 'gx')), may hold values from -0.1 to 0.12, as said below
Outputs:
- energy_next: float32 [256, 256, 1024], P('gz', 'gx', 'gy')
- plane_mean: float32 [256], P('gz')
- running_mean: float32 [256], P('gz')
Inputs may be any that keep to these rules, and one draw needn't show every extreme that they name: flow[0], flow[1] and flow[2] lie within -0.1 to 0.1; flow[3] lies within 0.02 to 0.12.
All inputs are finite; a program needn't handle non-finite values.
Results may differ from a plain program's by a relative error of at most 0.00002.
Values sent between devices are 32-bit elements; how exact they have to be, the bound alone decides.
A program may use at most 128 MiB of HBM per device.

v0:
```python
import jax
import jax.numpy as jnp
from jax import lax
from jax.sharding import PartitionSpec as P

directions = ((1, 0, 0), (0, 1, 0), (0, 0, 1))


def padded(x, sides, width):
    for axis, dim in sides:
        size, length = (lax.axis_size(axis), x.shape[dim])
        up = [(i, (i + 1) % size) for i in range(size)]
        down = [(j, i) for i, j in up]
        last = lax.slice_in_dim(x, length - width, length, axis=dim)
        first = lax.slice_in_dim(x, 0, width, axis=dim)
        before = lax.ppermute(last, axis, up)
        after = lax.ppermute(first, axis, down)
        x = jnp.concatenate([before, x, after], axis=dim)
    return x


def with_halo(x, sides, width):
    edges = {}
    for axis, dim in sides:
        size, length = (lax.axis_size(axis), x.shape[dim])
        up = [(i, (i + 1) % size) for i in range(size - 1)]
        last = lax.slice_in_dim(x, length - width, length, axis=dim)
        first = lax.slice_in_dim(x, 0, width, axis=dim)
        edges[dim] = (
            lax.ppermute(last, axis, up),
            lax.ppermute(first, axis, [(b, a) for a, b in up]),
        )
    done = []
    for _, dim in sides:
        low, high = edges[dim]
        around = [(width, width) if d in done else (0, 0) for d in range(x.ndim)]
        x = jnp.concatenate([jnp.pad(low, around), x, jnp.pad(high, around)], axis=dim)
        done.append(dim)
    return x


def in_blocks(x, dim, length):
    before, after = (x.shape[:dim], x.shape[dim + 1 :])
    return jnp.moveaxis(x.reshape(*before, length, -1, *after), dim, 0)


def in_order(tiles, dim):
    lengths = list(tiles.shape[1:])
    lengths[dim] *= tiles.shape[0]
    return jnp.moveaxis(tiles, 0, dim).reshape(lengths)


def one_exchange(x, axis, axes, splits, concats):
    sizes = [lax.axis_size(a) for a in axes]
    tiles = in_blocks(x, splits[0], sizes[0])
    tiles = jnp.moveaxis(in_blocks(tiles, splits[1] + 1, sizes[1]), 0, 1)
    inside = tiles.shape[2:]
    tiles = tiles.reshape(-1, *inside)
    tiles = lax.all_to_all(tiles, axis, split_axis=0, concat_axis=0, tiled=True)
    tiles = in_order(tiles.reshape(*sizes, *inside), concats[0] + 1)
    return in_order(tiles, concats[1])


def sent_to_all(x, axis):
    copies = jnp.broadcast_to(x, (lax.axis_size(axis), *x.shape))
    return lax.all_to_all(copies, axis, split_axis=0, concat_axis=0, tiled=True)


def taken_together(x, axis):
    return sent_to_all(x, axis).sum(axis=0)


def joined_by_halves(pieces, combine):
    while len(jax.tree.leaves(pieces)[0]) > 1:
        pieces = jax.vmap(combine)(*(pieces[side::2] for side in (0, 1)))
    return pieces[0]


def entering(x, axis, combine, identity):
    length, index = (lax.axis_size(axis), lax.axis_index(axis))
    passed = jnp.arange(length) < index

    def kept(part, zero, own):
        part = jnp.where(
            passed.reshape(-1, *(1 for _ in own.shape)), part, jnp.asarray(zero, own.dtype)
        )
        return part

    pieces = sent_to_all(x, axis)
    return joined_by_halves(kept(pieces, identity, x), combine)


def window(array, offset):
    return array[
        1 + offset[0] : array.shape[0] - 1 + offset[0],
        1 + offset[1] : array.shape[1] - 1 + offset[1],
        1 + offset[2] : array.shape[2] - 1 + offset[2],
    ]


def advance(energy_pad, kappa_pad, velocity):
    centre = window(energy_pad, (0, 0, 0))
    kappa_centre = window(kappa_pad, (0, 0, 0))
    change = jnp.zeros_like(centre)
    for axis_number, forward in enumerate(directions):
        backward = tuple((-item for item in forward))
        upper = window(energy_pad, forward)
        lower = window(energy_pad, backward)
        kappa_upper = window(kappa_pad, forward)
        kappa_lower = window(kappa_pad, backward)
        change = (
            change
            + 0.5 * (kappa_centre + kappa_upper) * (upper - centre)
            - 0.5 * (kappa_centre + kappa_lower) * (centre - lower)
        )
        speed = velocity[axis_number]
        change = (
            change
            - jnp.maximum(speed, 0.0) * (centre - lower)
            - jnp.minimum(speed, 0.0) * (upper - centre)
        )
    return centre + change


def fill_planes(stack):
    return padded(stack, (("gz", 1),), 1)


def fill_all(stack):
    sided = with_halo(stack, (("gx", 2), ("gy", 3)), 1)
    return fill_planes(sided)


def add_totals(earlier, later):
    return earlier + later


def per_device(energy, flow):
    fields = jnp.concatenate([energy[None], flow], 0)
    blocks = one_exchange(fields, ("gx", "gy"), ("gx", "gy"), (2, 3), (1, 1))
    velocity = blocks[1:4]
    pair_pad = fill_all(jnp.stack([blocks[0], blocks[4]]))
    kappa_pad = pair_pad[1]
    energy_half = advance(pair_pad[0], kappa_pad, velocity)
    half_pad = fill_all(energy_half[None])[0]
    energy_next = advance(half_pad, kappa_pad, velocity)
    local_sums = jnp.sum(energy_next, axis=(1, 2))
    plane_sums = taken_together(local_sums, ("gx", "gy"))
    cell_count = (
        energy_next.shape[1] * lax.axis_size("gx") * energy_next.shape[2] * lax.axis_size("gy")
    )
    plane_mean = plane_sums / cell_count
    block_total = jnp.sum(plane_mean)
    position = lax.axis_index("gz")
    offset = entering(block_total, "gz", add_totals, jnp.float32(0.0))
    planes_here = plane_mean.shape[0]
    ranks = (position * planes_here + jnp.arange(planes_here) + 1).astype(jnp.float32)
    running_mean = (offset + jnp.cumsum(plane_mean)) / ranks
    return (energy_next, plane_mean, running_mean)


def solution(mesh):
    placed = (P(("gz", "gy", "gx"), None, None), P(None, ("gz", "gy", "gx"), None, None))
    return jax.shard_map(
        per_device,
        mesh=mesh,
        in_specs=placed,
        out_specs=(P("gz", "gx", "gy"), P("gz"), P("gz")),
        check_vma=False,
    )
```

profile of v0, /device:TPU:24, one launch (start us, length us, event | category | flops | bytes accessed | tf_op | source)
XLA Modules:
  0.0 283.6 jit_solution(8078790732533910452)
XLA Ops:
  0.6 6.6 %copy.85 = f32[4,1,4,64,1024]{4,1,3,0,2:T(1,128)S(1)} copy(f32[4,1,4,64,1024]{4,3,2,0,1:T(8,128)} %bitcast.132) | data formatting | bytes 8388608 | tf_op jit(solution)/shard_map/concatenate | solution.py:139
  7.2 1.1 copy.84
  8.3 7.9 %pad_maximum_fusion = f32[5,1,4,64,1024]{4,1,3,0,2:T(1,128)S(1)} fusion(f32[4,1,4,64,1024]{4,1,3,0,2:T(1,128)S(1)} %copy.85, f32[1,1,4,64,1024]{4,1,3,0,2:T(1,128)S(1)} %copy.84), kind=kLoop, calls=%fused_computation | loop fusion | flops 1310720 | bytes 10485760 | tf_op jit(solution)/shard_map/concatenate | solution.py:139
  16.3 0.9 copy.86
  17.2 126.3 %all_to_all.20 = f32[32,5,1,64,128]{4,3,1,2,0:T(8,128)S(1)} all-to-all(f32[32,5,1,64,128]{4,3,1,2,0:T(8,128)S(1)} %bitcast.131), channel_id=1, replica_groups=mesh['gx'=4,'gy'=8,'gz'=8] {'gx','gy'}, dimensions={0} | all-to-all | bytes 10485760 | tf_op jit(solution)/shard_map/all_to_all | solution.py:59
  143.5 2.6 fusion.34
  146.3 1.3 collective-permute-start.2
  147.6 4.5 %collective-permute-start.1 = (f32[2,32,1,128]{3,2,1,0:T(1,128)S(1)}, f32[2,32,1,128]{3,2,1,0:T(1,128)S(1)}, u32[]{:S(2)}, u32[]{:S(2)}) collective-permute-start(f32[2,32,1,128]{3,2,1,0:T(1,128)S(1)} %get-tuple-element.21), channel_id=1, source_target_pairs={{0,64},{64,128},{128,192},{1,65},{65,129},{129,193},{2,66},{66,130... | collective-permute-start | bytes 98312 | tf_op jit(solution)/shard_map/ppermute | solution.py:30
  152.2 2.7 fusion
  154.9 2.3 copy.92
  157.1 1.3 collective-permute-start.3
  158.5 2.3 copy.90
  160.7 3.2 %collective-permute-start = (f32[2,32,64,1]{2,1,3,0:T(8,128)S(1)}, f32[2,32,64,1]{2,1,3,0:T(8,128)S(1)}, u32[]{:S(2)}, u32[]{:S(2)}) collective-permute-start(f32[2,32,64,1]{2,1,3,0:T(8,128)S(1)} %copy.90), channel_id=1, source_target_pairs={{0,8},{8,16},{16,24},{24,32},{32,40},{40,48},{48,56},{1,9},{9,17},... | collective-permute-start | bytes 49160 | tf_op jit(solution)/shard_map/ppermute | solution.py:30
  164.0 2.0 copy.93
  166.0 3.3 %pad.15 = f32[2,32,66,1]{3,2,1,0:T(8,128)} pad(f32[2,32,64,1]{3,2,1,0:T(8,128)} %copy.93, f32[]{:T(128)} %constant.6.clone.1), padding=0_0x0_0x1_1x0_0 | pad | bytes 33284 | tf_op jit(solution)/shard_map/jit(_pad)/pad | solution.py:37
  169.2 2.0 copy.91
  171.3 2.0 pad.14
  173.8 4.7 %collective-permute-start.5 = (f32[2,1,66,130]{3,2,1,0:T(8,128)S(1)}, f32[2,1,66,130]{3,2,1,0:T(8,128)S(1)}, u32[]{:S(2)}, u32[]{:S(2)}) collective-permute-start(f32[2,1,66,130]{3,2,1,0:T(8,128)S(1)} %get-tuple-element.8), channel_id=1, source_target_pairs={{1,0},{2,1},{3,2},{4,3},{5,4},{6,5},{7,6},{0,7},{9,8},{10,9},{11,1... | collective-permute-start | bytes 205928 | tf_op jit(solution)/shard_map/ppermute | solution.py:17
  178.5 1.3 collective-permute-start.4
  180.1 1.8 copy-done.15
  182.7 5.8 %collective-permute-done.5 = f32[2,1,66,130]{3,2,1,0:T(8,128)S(1)} collective-permute-done((f32[2,1,66,130]{3,2,1,0:T(8,128)S(1)}, f32[2,1,66,130]{3,2,1,0:T(8,128)S(1)}, u32[]{:S(2)}, u32[]{:S(2)}) %collective-permute-start.5) | collective-permute-done | bytes 68672 | tf_op jit(solution)/shard_map/ppermute | solution.py:17
  188.6 5.6 %collective-permute-done.4 = f32[2,1,66,130]{3,2,1,0:T(8,128)S(1)} collective-permute-done((f32[2,1,66,130]{3,2,1,0:T(8,128)S(1)}, f32[2,1,66,130]{3,2,1,0:T(8,128)S(1)}, u32[]{:S(2)}, u32[]{:S(2)}) %collective-permute-start.4) | collective-permute-done | bytes 68672 | tf_op jit(solution)/shard_map/ppermute | solution.py:16
  194.1 4.4 %pad_maximum_fusion.1 = f32[2,34,66,130]{3,2,1,0:T(8,128)S(1)} fusion(f32[2,1,66,130]{3,2,1,0:T(8,128)S(1)} %collective-permute-done.5, f32[2,32,66,1]{3,2,1,0:T(8,128)S(1)} %copy-done, f32[2,32,1,128]{3,2,1,0:T(1,128)S(1)} %collective-permute-done.2, f32[1,32,64,128]{3,2,1,0:T(8,128)S(1)} %bitcast.128, f32[1,32,64,128]{3,2,1,0:T(8,128)S(1)} %bitcast.124, ...), kind=kLoop, calls=%fused_computation.1 | loop fusion | flops 4084080 | bytes 4667520 | tf_op jit(solution)/shard_map/concatenate | solution.py:18
  199.1 4.3 %fusion.8 = f32[32,64,128]{2,1,0:T(8,128)S(1)} fusion(f32[1,8,4,64,128]{4,3,2,1,0:T(8,128)S(1)} %copy.99, f32[1,8,4,64,128]{4,3,2,1,0:T(8,128)S(1)} %copy.98, f32[1,8,4,64,128]{4,3,2,1,0:T(8,128)S(1)} %copy.97, f32[1,8,4,64,128]{4,3,2,1,0:T(8,128)S(1)} %copy.96, f32[1,8,4,64,128]{4,3,2,1,0:T(8,128)S(1)} %copy.95, f32[1,8,4,64,128]{4,3,2,1,0:T(8,128)S(1)} %copy.94, ...), kind=kLoop, calls=%fused_computation.40 | loop fusion | flops 11010048 | bytes 22020096 | tf_op jit(solution)/shard_map/add | solution.py:122
  203.3 0.6 fusion.35
  204.0 1.3 collective-permute-start.8
  205.3 5.1 %collective-permute-start.7 = (f32[1,32,1,128]{3,2,1,0:T(1,128)}, f32[1,32,1,128]{3,2,1,0:T(1,128)}, u32[]{:S(2)}, u32[]{:S(2)}) collective-permute-start(f32[1,32,1,128]{3,2,1,0:T(1,128)} %get-tuple-element.25), channel_id=1, source_target_pairs={{0,64},{64,128},{128,192},{1,65},{65,129},{129,193},{2,66},{66,130... | collective-permute-start | bytes 49160 | tf_op jit(solution)/shard_map/ppermute | solution.py:30
  210.4 1.7 fusion.36
  212.1 2.2 copy.102
  214.3 1.3 collective-permute-start.9
  215.6 2.2 copy.100
  217.8 3.6 %collective-permute-start.6 = (f32[1,32,64,1]{2,1,3,0:T(8,128)}, f32[1,32,64,1]{2,1,3,0:T(8,128)}, u32[]{:S(2)}, u32[]{:S(2)}) collective-permute-start(f32[1,32,64,1]{2,1,3,0:T(8,128)} %copy.100), channel_id=1, source_target_pairs={{0,8},{8,16},{16,24},{24,32},{32,40},{40,48},{48,56},{1,9},{9,17},... | collective-permute-start | bytes 24584 | tf_op jit(solution)/shard_map/ppermute | solution.py:30
  221.4 2.1 copy.103
  223.5 2.4 pad.17
  225.9 2.1 copy.101
  228.0 1.4 pad.16
  229.5 0.9 pad_maximum_fusion.13
  230.5 1.9 collective-permute-start.11
  232.4 4.4 %collective-permute-start.10 = (f32[1,1,66,130]{3,2,1,0:T(8,128)S(1)}, f32[1,1,66,130]{3,2,1,0:T(8,128)S(1)}, u32[]{:S(2)}, u32[]{:S(2)}) collective-permute-start(f32[1,1,66,130]{3,2,1,0:T(8,128)S(1)} %get-tuple-element.19), channel_id=1, source_target_pairs={{0,1},{1,2},{2,3},{3,4},{4,5},{5,6},{6,7},{7,0},{8,9},{9,10},{10,1... | collective-permute-start | bytes 102968 | tf_op jit(solution)/shard_map/ppermute | solution.py:16
  236.8 3.8 %collective-permute-done.11 = f32[1,1,66,130]{3,2,1,0:T(8,128)S(1)} collective-permute-done((f32[1,1,66,130]{3,2,1,0:T(8,128)S(1)}, f32[1,1,66,130]{3,2,1,0:T(8,128)S(1)}, u32[]{:S(2)}, u32[]{:S(2)}) %collective-permute-start.11) | collective-permute-done | bytes 34352 | tf_op jit(solution)/shard_map/ppermute | solution.py:17
  240.5 2.0 collective-permute-done.10
  242.6 1.9 maximum_bitcast_fusion
  244.5 5.4 %fusion.32 = (f32[32]{0:T(128)S(1)}, f32[32,64,128]{2,1,0:T(8,128)}) fusion(f32[1,8,4,64,128]{4,3,2,1,0:T(8,128)S(1)} %copy-done.3, f32[1,8,4,64,128]{4,3,2,1,0:T(8,128)S(1)} %copy-done.5, f32[34,66,130]{2,1,0:T(8,128)S(1)} %maximum_bitcast_fusion, f32[34,66,130]{2,1,0:T(8,128)S(1)} %get-tuple-element.17, f32[1,8,4,64,128]{4,3,2,1,0:T(8,128)S(1)} %copy-done.7, ...), kind=kLoop, calls=%fused_computation.95 | loop fusion | flops 11272160 | bytes 22020224 | tf_op jit(solution)/shard_map/reduce_sum | solution.py:147
  250.5 4.0 %all-to-all-start.1 = ((f32[32,1,32]{2,1,0:T(1,128)}), f32[32,1,32]{2,1,0:T(1,128)S(1)}, u32[]{:S(2)}, u32[]{:S(2)}) async-start(f32[32,1,32]{2,1,0:T(1,128)} %broadcast_in_dim.15), calls=%async_computation.1 | async-start | bytes 32768 | tf_op jit(solution)/shard_map/all_to_all | solution.py:66
  254.5 7.7 %all-to-all-done.1 = f32[32,1,32]{2,1,0:T(1,128)S(1)} async-done(((f32[32,1,32]{2,1,0:T(1,128)}), f32[32,1,32]{2,1,0:T(1,128)S(1)}, u32[]{:S(2)}, u32[]{:S(2)}) %all-to-all-start.1) | async-done | bytes 4128 | tf_op jit(solution)/shard_map/all_to_all | solution.py:66
  263.0 1.2 broadcast_in_dim.16
  264.2 8.3 %all-to-all-start.2 = ((f32[8,1,1]{2,1,0:T(1,128)}), f32[8,1,1]{2,1,0:T(1,128)S(1)}, u32[]{:S(2)}, u32[]{:S(2)}) async-start(f32[8,1,1]{2,1,0:T(1,128)} %broadcast_in_dim.16), calls=%async_computation.2 | async-start | bytes 8192 | tf_op jit(solution)/shard_map/all_to_all | solution.py:66
  272.6 8.0 %all-to-all-done.2 = f32[8,1,1]{2,1,0:T(1,128)S(1)} async-done(((f32[8,1,1]{2,1,0:T(1,128)}), f32[8,1,1]{2,1,0:T(1,128)S(1)}, u32[]{:S(2)}, u32[]{:S(2)}) %all-to-all-start.2) | async-done | bytes 64 | tf_op jit(solution)/shard_map/all_to_all | solution.py:66
  (76 shorter events, 5.5 us)
Async XLA Ops:
  0.6 6.6 %copy-start.19 = (f32[1,256,1024]{2,1,0:T(8,128)S(1)}, f32[1,256,1024]{2,1,0:T(8,128)}, u32[]{:S(2)}) copy-start(f32[1,256,1024]{2,1,0:T(8,128)} %param.2) | copy-start | bytes 3145732
  146.3 27.0 %collective-permute-start.2 = (f32[2,32,1,128]{3,2,1,0:T(1,128)S(1)}, f32[2,32,1,128]{3,2,1,0:T(1,128)S(1)}, u32[]{:S(2)}, u32[]{:S(2)}) collective-permute-start(f32[2,32,1,128]{3,2,1,0:T(1,128)S(1)} %get-tuple-element.22), channel_id=1, source_target_pairs={{64,0},{128,64},{192,128},{65,1},{129,65},{193,129},{66,2},{130,66... | collective-permute-start | bytes 98312 | tf_op jit(solution)/shard_map/ppermute | solution.py:31
  147.6 25.7 %collective-permute-start.1 = (f32[2,32,1,128]{3,2,1,0:T(1,128)S(1)}, f32[2,32,1,128]{3,2,1,0:T(1,128)S(1)}, u32[]{:S(2)}, u32[]{:S(2)}) collective-permute-start(f32[2,32,1,128]{3,2,1,0:T(1,128)S(1)} %get-tuple-element.21), channel_id=1, source_target_pairs={{0,64},{64,128},{128,192},{1,65},{65,129},{129,193},{2,66},{66,130... | collective-permute-start | bytes 98312 | tf_op jit(solution)/shard_map/ppermute | solution.py:30
  157.1 6.8 %collective-permute-start.3 = (f32[2,32,64,1]{2,1,3,0:T(8,128)S(1)}, f32[2,32,64,1]{2,1,3,0:T(8,128)S(1)}, u32[]{:S(2)}, u32[]{:S(2)}) collective-permute-start(f32[2,32,64,1]{2,1,3,0:T(8,128)S(1)} %copy.92), channel_id=1, source_target_pairs={{8,0},{16,8},{24,16},{32,24},{40,32},{48,40},{56,48},{9,1},{17,9},... | collective-permute-start | bytes 49160 | tf_op jit(solution)/shard_map/ppermute | solution.py:31
  160.7 8.5 %collective-permute-start = (f32[2,32,64,1]{2,1,3,0:T(8,128)S(1)}, f32[2,32,64,1]{2,1,3,0:T(8,128)S(1)}, u32[]{:S(2)}, u32[]{:S(2)}) collective-permute-start(f32[2,32,64,1]{2,1,3,0:T(8,128)S(1)} %copy.90), channel_id=1, source_target_pairs={{0,8},{8,16},{16,24},{24,32},{32,40},{40,48},{48,56},{1,9},{9,17},... | collective-permute-start | bytes 49160 | tf_op jit(solution)/shard_map/ppermute | solution.py:30
  171.3 2.3 copy-start
  173.3 6.5 %copy-start.18 = (f32[1,8,4,64,128]{4,3,0,1,2:T(8,128)S(1)}, f32[1,8,4,64,128]{4,3,0,1,2:T(8,128)}, u32[]{:S(2)}) copy-start(f32[1,8,4,64,128]{4,3,0,1,2:T(8,128)} %get-tuple-element.12) | copy-start | bytes 3145732
  173.8 6.1 %copy-start.17 = (f32[1,8,4,64,128]{4,3,0,1,2:T(8,128)S(1)}, f32[1,8,4,64,128]{4,3,0,1,2:T(8,128)}, u32[]{:S(2)}) copy-start(f32[1,8,4,64,128]{4,3,0,1,2:T(8,128)} %get-tuple-element.13) | copy-start | bytes 3145732
  173.8 6.2 %copy-start.16 = (f32[1,8,4,64,128]{4,3,0,1,2:T(8,128)S(1)}, f32[1,8,4,64,128]{4,3,0,1,2:T(8,128)}, u32[]{:S(2)}) copy-start(f32[1,8,4,64,128]{4,3,0,1,2:T(8,128)} %get-tuple-element.11) | copy-start | bytes 3145732
  173.8 14.8 %collective-permute-start.5 = (f32[2,1,66,130]{3,2,1,0:T(8,128)S(1)}, f32[2,1,66,130]{3,2,1,0:T(8,128)S(1)}, u32[]{:S(2)}, u32[]{:S(2)}) collective-permute-start(f32[2,1,66,130]{3,2,1,0:T(8,128)S(1)} %get-tuple-element.8), channel_id=1, source_target_pairs={{1,0},{2,1},{3,2},{4,3},{5,4},{6,5},{7,6},{0,7},{9,8},{10,9},{11,1... | collective-permute-start | bytes 205928 | tf_op jit(solution)/shard_map/ppermute | solution.py:17
  178.5 15.6 %collective-permute-start.4 = (f32[2,1,66,130]{3,2,1,0:T(8,128)S(1)}, f32[2,1,66,130]{3,2,1,0:T(8,128)S(1)}, u32[]{:S(2)}, u32[]{:S(2)}) collective-permute-start(f32[2,1,66,130]{3,2,1,0:T(8,128)S(1)} %get-tuple-element.7), channel_id=1, source_target_pairs={{0,1},{1,2},{2,3},{3,4},{4,5},{5,6},{6,7},{7,0},{8,9},{9,10},{10,1... | collective-permute-start | bytes 205928 | tf_op jit(solution)/shard_map/ppermute | solution.py:16
  179.9 19.1 %copy-start.2 = (f32[1,8,4,64,128]{4,3,2,1,0:T(8,128)}, f32[1,8,4,64,128]{4,3,2,1,0:T(8,128)S(1)}, u32[]{:S(2)}) copy-start(f32[1,8,4,64,128]{4,3,2,1,0:T(8,128)S(1)} %copy.99) | copy-start | bytes 3145732
  179.9 2.0 copy-start.15
  180.0 19.0 %copy-start.4 = (f32[1,8,4,64,128]{4,3,2,1,0:T(8,128)}, f32[1,8,4,64,128]{4,3,2,1,0:T(8,128)S(1)}, u32[]{:S(2)}) copy-start(f32[1,8,4,64,128]{4,3,2,1,0:T(8,128)S(1)} %copy.98) | copy-start | bytes 3145732
  180.0 2.6 copy-start.14
  180.1 18.9 %copy-start.6 = (f32[1,8,4,64,128]{4,3,2,1,0:T(8,128)}, f32[1,8,4,64,128]{4,3,2,1,0:T(8,128)S(1)}, u32[]{:S(2)}) copy-start(f32[1,8,4,64,128]{4,3,2,1,0:T(8,128)S(1)} %copy.97) | copy-start | bytes 3145732
  182.0 17.1 %copy-start.8 = (f32[1,8,4,64,128]{4,3,2,1,0:T(8,128)}, f32[1,8,4,64,128]{4,3,2,1,0:T(8,128)S(1)}, u32[]{:S(2)}) copy-start(f32[1,8,4,64,128]{4,3,2,1,0:T(8,128)S(1)} %copy.96) | copy-start | bytes 3145732
  182.6 16.4 %copy-start.10 = (f32[1,8,4,64,128]{4,3,2,1,0:T(8,128)}, f32[1,8,4,64,128]{4,3,2,1,0:T(8,128)S(1)}, u32[]{:S(2)}) copy-start(f32[1,8,4,64,128]{4,3,2,1,0:T(8,128)S(1)} %copy.95) | copy-start | bytes 3145732
  182.7 16.3 %copy-start.12 = (f32[1,8,4,64,128]{4,3,2,1,0:T(8,128)}, f32[1,8,4,64,128]{4,3,2,1,0:T(8,128)S(1)}, u32[]{:S(2)}) copy-start(f32[1,8,4,64,128]{4,3,2,1,0:T(8,128)S(1)} %copy.94) | copy-start | bytes 3145732
  204.0 25.4 %collective-permute-start.8 = (f32[1,32,1,128]{3,2,1,0:T(1,128)}, f32[1,32,1,128]{3,2,1,0:T(1,128)}, u32[]{:S(2)}, u32[]{:S(2)}) collective-permute-start(f32[1,32,1,128]{3,2,1,0:T(1,128)} %get-tuple-element.26), channel_id=1, source_target_pairs={{64,0},{128,64},{192,128},{65,1},{129,65},{193,129},{66,2},{130,66... | collective-permute-start | bytes 49160 | tf_op jit(solution)/shard_map/ppermute | solution.py:31
  205.3 24.1 %collective-permute-start.7 = (f32[1,32,1,128]{3,2,1,0:T(1,128)}, f32[1,32,1,128]{3,2,1,0:T(1,128)}, u32[]{:S(2)}, u32[]{:S(2)}) collective-permute-start(f32[1,32,1,128]{3,2,1,0:T(1,128)} %get-tuple-element.25), channel_id=1, source_target_pairs={{0,64},{64,128},{128,192},{1,65},{65,129},{129,193},{2,66},{66,130... | collective-permute-start | bytes 49160 | tf_op jit(solution)/shard_map/ppermute | solution.py:30
  214.3 7.1 %collective-permute-start.9 = (f32[1,32,64,1]{2,1,3,0:T(8,128)}, f32[1,32,64,1]{2,1,3,0:T(8,128)}, u32[]{:S(2)}, u32[]{:S(2)}) collective-permute-start(f32[1,32,64,1]{2,1,3,0:T(8,128)} %copy.102), channel_id=1, source_target_pairs={{8,0},{16,8},{24,16},{32,24},{40,32},{48,40},{56,48},{9,1},{17,9},... | collective-permute-start | bytes 24584 | tf_op jit(solution)/shard_map/ppermute | solution.py:31
  217.8 8.1 %collective-permute-start.6 = (f32[1,32,64,1]{2,1,3,0:T(8,128)}, f32[1,32,64,1]{2,1,3,0:T(8,128)}, u32[]{:S(2)}, u32[]{:S(2)}) collective-permute-start(f32[1,32,64,1]{2,1,3,0:T(8,128)} %copy.100), channel_id=1, source_target_pairs={{0,8},{8,16},{16,24},{24,32},{32,40},{40,48},{48,56},{1,9},{9,17},... | collective-permute-start | bytes 24584 | tf_op jit(solution)/shard_map/ppermute | solution.py:30
  228.0 1.6 copy-start.1
  229.5 14.9 %copy-start.13 = (f32[1,8,4,64,128]{4,3,2,1,0:T(8,128)S(1)}, f32[1,8,4,64,128]{4,3,2,1,0:T(8,128)}, u32[]{:S(2)}) copy-start(f32[1,8,4,64,128]{4,3,2,1,0:T(8,128)} %copy-done.12) | copy-start | bytes 3145732
  230.5 10.1 %collective-permute-start.11 = (f32[1,1,66,130]{3,2,1,0:T(8,128)S(1)}, f32[1,1,66,130]{3,2,1,0:T(8,128)S(1)}, u32[]{:S(2)}, u32[]{:S(2)}) collective-permute-start(f32[1,1,66,130]{3,2,1,0:T(8,128)S(1)} %get-tuple-element.20), channel_id=1, source_target_pairs={{1,0},{2,1},{3,2},{4,3},{5,4},{6,5},{7,6},{0,7},{9,8},{10,9},{11,1... | collective-permute-start | bytes 102968 | tf_op jit(solution)/shard_map/ppermute | solution.py:17
  232.3 12.1 %copy-start.3 = (f32[1,8,4,64,128]{4,3,2,1,0:T(8,128)S(1)}, f32[1,8,4,64,128]{4,3,2,1,0:T(8,128)}, u32[]{:S(2)}) copy-start(f32[1,8,4,64,128]{4,3,2,1,0:T(8,128)} %copy-done.2) | copy-start | bytes 3145732
  232.3 12.1 %copy-start.5 = (f32[1,8,4,64,128]{4,3,2,1,0:T(8,128)S(1)}, f32[1,8,4,64,128]{4,3,2,1,0:T(8,128)}, u32[]{:S(2)}) copy-start(f32[1,8,4,64,128]{4,3,2,1,0:T(8,128)} %copy-done.4) | copy-start | bytes 3145732
  232.3 12.2 %copy-start.7 = (f32[1,8,4,64,128]{4,3,2,1,0:T(8,128)S(1)}, f32[1,8,4,64,128]{4,3,2,1,0:T(8,128)}, u32[]{:S(2)}) copy-start(f32[1,8,4,64,128]{4,3,2,1,0:T(8,128)} %copy-done.6) | copy-start | bytes 3145732
  232.3 12.2 %copy-start.9 = (f32[1,8,4,64,128]{4,3,2,1,0:T(8,128)S(1)}, f32[1,8,4,64,128]{4,3,2,1,0:T(8,128)}, u32[]{:S(2)}) copy-start(f32[1,8,4,64,128]{4,3,2,1,0:T(8,128)} %copy-done.8) | copy-start | bytes 3145732
  232.4 12.2 %copy-start.11 = (f32[1,8,4,64,128]{4,3,2,1,0:T(8,128)S(1)}, f32[1,8,4,64,128]{4,3,2,1,0:T(8,128)}, u32[]{:S(2)}) copy-start(f32[1,8,4,64,128]{4,3,2,1,0:T(8,128)} %copy-done.10) | copy-start | bytes 3145732
  232.4 10.2 %collective-permute-start.10 = (f32[1,1,66,130]{3,2,1,0:T(8,128)S(1)}, f32[1,1,66,130]{3,2,1,0:T(8,128)S(1)}, u32[]{:S(2)}, u32[]{:S(2)}) collective-permute-start(f32[1,1,66,130]{3,2,1,0:T(8,128)S(1)} %get-tuple-element.19), channel_id=1, source_target_pairs={{0,1},{1,2},{2,3},{3,4},{4,5},{5,6},{6,7},{7,0},{8,9},{9,10},{10,1... | collective-permute-start | bytes 102968 | tf_op jit(solution)/shard_map/ppermute | solution.py:16
  250.5 11.7 %all-to-all-start.1 = ((f32[32,1,32]{2,1,0:T(1,128)}), f32[32,1,32]{2,1,0:T(1,128)S(1)}, u32[]{:S(2)}, u32[]{:S(2)}) async-start(f32[32,1,32]{2,1,0:T(1,128)} %broadcast_in_dim.15), calls=%async_computation.1 | async-start | bytes 32768 | tf_op jit(solution)/shard_map/all_to_all | solution.py:66
  262.9 20.7 %copy-start.20 = (f32[32]{0:T(128)}, f32[32]{0:T(128)S(1)}, u32[]{:S(2)}) copy-start(f32[32]{0:T(128)S(1)} %get-tuple-element.4) | copy-start | bytes 388
  264.2 16.3 %all-to-all-start.2 = ((f32[8,1,1]{2,1,0:T(1,128)}), f32[8,1,1]{2,1,0:T(1,128)S(1)}, u32[]{:S(2)}, u32[]{:S(2)}) async-start(f32[8,1,1]{2,1,0:T(1,128)} %broadcast_in_dim.16), calls=%async_computation.2 | async-start | bytes 8192 | tf_op jit(solution)/shard_map/all_to_all | solution.py:66
where the time goes:
time: 286 us; the launch traced here: 284 us
  blocking collectives  126 us (44%)
  starting transfers between devices  46.3 us (16%)
  local copies, waits for them, and re-layouts  43.9 us (15%)
  waiting for transfers between devices  32.9 us (12%)
  other arithmetic  31.9 us (11%)
    all_to_all x1, blocking collectives, one_exchange(): tiles = lax.all_to_all(tiles, axis, split_axis=0, concat_axis=0, tiled=True)  126 us
    ppermute x4, starting transfers between devices, with_halo(): lax.ppermute(last, axis, up)  16.5 us
    all_to_all x2, waiting for transfers between devices, sent_to_all(): return lax.all_to_all(copies, axis, split_axis=0, concat_axis=0, tiled=True)  15.7 us
    all_to_all x2, starting transfers between devices, sent_to_all(): return lax.all_to_all(copies, axis, split_axis=0, concat_axis=0, tiled=True)  12.3 us
    ppermute x2, waiting for transfers between devices, padded(): after = lax.ppermute(first, axis, down)  9.57 us
    concatenate x1, other arithmetic, per_device(): fields = jnp.concatenate([energy[None], flow], 0)  7.91 us
    concatenate x2, local copies, waits for them, and re-layouts, per_device(): fields = jnp.concatenate([energy[None], flow], 0)  7.67 us
    ppermute x2, waiting for transfers between devices, padded(): before = lax.ppermute(last, axis, up)  7.61 us
  transfers between devices with their start and end apart: 14, of which 6 were waited for; matrix products, arithmetic and copies ran while one was open for 11% of the time, Pallas kernels for 0%

commit v1 on v0

v1 whole, which is shorter than its diff:
```python
import functools

import jax
import jax.numpy as jnp
from jax import lax
from jax.experimental import pallas as pl
from jax.experimental.pallas import tpu as pltpu
from jax.sharding import PartitionSpec as P

MESH = pl.DeviceIdType.MESH
AHEAD = 3


def change_of(X, p, xi, F, fi):
    here = X[p, :, pl.ds(xi, 8), :]
    kappa = F[3, p, :, pl.ds(fi, 8), :]
    lane = lax.broadcasted_iota(jnp.int32, here.shape, 2)
    none = jnp.zeros_like(here[:1])

    def right(v):
        r = pltpu.roll(v, 127, 2)
        return jnp.where(lane == 127, jnp.concatenate([r[1:], none], 0), r)

    def left(v):
        r = pltpu.roll(v, 1, 2)
        return jnp.where(lane == 0, jnp.concatenate([none, r[:-1]], 0), r)

    sides = (
        (
            0,
            X[p + 1, :, pl.ds(xi, 8), :],
            F[3, p + 1, :, pl.ds(fi, 8), :],
            X[p - 1, :, pl.ds(xi, 8), :],
            F[3, p - 1, :, pl.ds(fi, 8), :],
        ),
        (
            1,
            X[p, :, pl.ds(xi + 1, 8), :],
            F[3, p, :, pl.ds(fi + 1, 8), :],
            X[p, :, pl.ds(xi - 1, 8), :],
            F[3, p, :, pl.ds(fi - 1, 8), :],
        ),
        (2, right(here), right(kappa), left(here), left(kappa)),
    )
    change = jnp.zeros_like(here)
    for axis, upper, kappa_upper, lower, kappa_lower in sides:
        speed = F[axis, p, :, pl.ds(fi, 8), :]
        change = (
            change
            + (0.5 * (kappa + kappa_upper) - jnp.minimum(speed, 0.0)) * (upper - here)
            - (0.5 * (kappa + kappa_lower) + jnp.maximum(speed, 0.0)) * (here - lower)
        )
    return here + change


def kernel(
    nx, ny, nz, e_ref, f_ref, o_ref, pm_ref, rm_ref, E, F, H, N, acc, SA, SB, SC, SM,
    xsE, xsF, xrE, xrF, gsE, gsK, gsU, grE, grK, grU, zsE, zsK, zsH, zrE, zrK, zrH,
    osem, orem, sa_s, sa_r, sb_s, sb_r, sc_s, sc_r, tok,
):
    gx, gy, gz = (lax.axis_index(a) for a in ("gx", "gy", "gz"))
    ring = ny * nz
    m = gz * ny + gy
    up, down = lax.rem(m + 1, ring), lax.rem(m + ring - 1, ring)
    chain = tuple({"gy": lax.rem(n, ny), "gz": n // ny} for n in (up, down))
    rows = 64
    tiles = rows // 8

    bar = pltpu.get_barrier_semaphore()
    for d in range(1, nx):
        pl.semaphore_signal(
            bar, inc=1, device_id={"gx": lax.rem(gx + d, nx)}, device_id_type=MESH
        )
    for to in chain:
        pl.semaphore_signal(bar, inc=1, device_id=to, device_id_type=MESH)

    def copy(src, dst, send, recv, to):
        return pltpu.make_async_remote_copy(
            src_ref=src, dst_ref=dst, send_sem=send, recv_sem=recv, device_id=to,
            device_id_type=MESH,
        )

    def x_tile(d, c):
        t = lax.rem(gx + d, nx)
        src = (e_ref.at[t * tiles + c], f_ref.at[:, t * tiles + c])
        at = pl.ds(pl.multiple_of(8 + 8 * c, 8), 8)
        dst = (E.at[1 + gx, :, at, :], F.at[:, 1 + gx, :, at, :])
        if d == 0:
            return (
                pltpu.make_async_copy(src[0], dst[0], xrE.at[0, c]),
                pltpu.make_async_copy(src[1], dst[1], xrF.at[0, c]),
            )
        return (
            copy(src[0], dst[0], xsE.at[d], xrE.at[d, c], {"gx": t}),
            copy(src[1], dst[1], xsF.at[d], xrF.at[d, c], {"gx": t}),
        )

    def x_edge(d, side):
        t = lax.rem(gx + d, nx)
        if side == 0:
            tile = lax.max(t * tiles - 1, 0)
            wide, narrow, wide_at, narrow_at = pl.ds(6, 2), pl.ds(7, 1), pl.ds(6, 2), pl.ds(7, 1)
        else:
            tile = lax.min((t + 1) * tiles, nx * tiles - 1)
            wide, narrow = pl.ds(0, 2), pl.ds(0, 1)
            wide_at, narrow_at = pl.ds(8 + rows, 2), pl.ds(8 + rows, 1)
        parts = (
            (e_ref.at[tile, :, wide, :], E.at[1 + gx, :, wide_at, :], gsE, grE),
            (f_ref.at[3, tile, :, wide, :], F.at[3, 1 + gx, :, wide_at, :], gsK, grK),
            (
                f_ref.at[pl.ds(0, 3), tile, :, narrow, :],
                F.at[pl.ds(0, 3), 1 + gx, :, narrow_at, :],
                gsU,
                grU,
            ),
        )
        if d == 0:
            return [pltpu.make_async_copy(a, b, r.at[0, side]) for a, b, s, r in parts]
        return [copy(a, b, s.at[d, side], r.at[d, side], {"gx": t}) for a, b, s, r in parts]

    def has_edge(g, side):
        return g > 0 if side == 0 else g < nx - 1

    def start_tile(c):
        for d in (0, *range(1, nx)):
            for x in x_tile(d, c):
                x.start()

    def start_edges(side):
        for d in range(nx):

            @pl.when(has_edge(lax.rem(gx + d, nx), side))
            def _():
                for x in x_edge(d, side):
                    x.start()

    def z_window(way, at, c):
        src, dst = ((4, 0), (1, 5))[way]
        return (
            copy(E.at[src, :, at, :], E.at[dst, :, at, :], zsE.at[way], zrE.at[way, c], chain[way]),
            copy(
                F.at[3, src, :, at, :], F.at[3, dst, :, at, :], zsK.at[way], zrK.at[way, c],
                chain[way],
            ),
        )

    def h_window(way, at, c):
        src, dst = ((4, 0), (1, 5))[way]
        return copy(
            H.at[src, :, at, :], H.at[dst, :, at, :], zsH.at[way], zrH.at[way, c], chain[way]
        )

    def out_window(d, src_at, dst_at):
        t = lax.rem(gy + d, ny)
        return copy(
            N.at[:, t, src_at, :], o_ref.at[pl.ds(4 * gy, 4), dst_at, :], osem.at[d], orem.at[d],
            {"gy": t},
        )

    def send_out(src_at, dst_at):
        def one(d, _):
            out_window(d, src_at, dst_at).start()
            return 0

        lax.fori_loop(1, ny, one, 0)
        pltpu.make_async_copy(
            N.at[:, gy, src_at, :], o_ref.at[pl.ds(4 * gy, 4), dst_at, :], orem.at[0]
        ).start()

    def half(c):
        def plane(p, _):
            v = change_of(E, p, 8 * c + 7, F, 8 * c + 7)
            r = lax.broadcasted_iota(jnp.int32, v.shape, 1) + (8 * c - 1 + rows * gx)
            H[p, :, pl.ds(pl.multiple_of(8 * c + 8, 8), 8), :] = jnp.where(
                (r >= 0) & (r < rows * nx), v, 0.0
            )
            return 0

        lax.fori_loop(1, 5, plane, 0)

    def full(c):
        def plane(p, _):
            v = change_of(H, p, 8 * c + 7, F, 8 * c + 6)
            N[p - 1, :, pl.ds(pl.multiple_of(8 * c, 8), 8), :] = v
            r = lax.broadcasted_iota(jnp.int32, v.shape, 1) + (8 * c - 2)
            acc[p - 1] += jnp.sum(jnp.where((r >= 0) & (r < rows), v, 0.0), axis=0)
            return 0

        lax.fori_loop(1, 5, plane, 0)

    def wait_tile(c):
        for d in range(nx):
            for x in x_tile(d, c):
                x.wait() if d == 0 else x.wait_recv()

    def wait_edges(side):
        @pl.when(has_edge(gx, side))
        def _():
            for d in range(nx):
                for x in x_edge(d, side):
                    x.wait() if d == 0 else x.wait_recv()

    def body_at(c):
        return pl.ds(pl.multiple_of(8 * c, 8), 8), pl.ds(8 * c - 2, 8)

    first_at = (pl.ds(2, 6), pl.ds(0, 6))

    acc[...] = jnp.zeros_like(acc)
    for side, at in ((0, slice(6, 8)), (1, slice(8 + rows, 10 + rows))):

        @pl.when(jnp.logical_not(has_edge(gx, side)))
        def _():
            E[1:5, :, at, :] = jnp.zeros_like(E[1:5, :, at, :])
            F[3, 1:5, :, at, :] = jnp.zeros_like(E[1:5, :, at, :])

    pl.semaphore_wait(bar, nx + 1)
    start_edges(0)
    start_tile(0)
    start_edges(1)
    for c in range(1, AHEAD):
        start_tile(c)
    wait_edges(0)

    def step(c, _):
        @pl.when(c + AHEAD < tiles)
        def _():
            start_tile(c + AHEAD)

        wait_tile(c)
        at = pl.ds(8 * c + 7, 8)
        for way in (0, 1):
            for x in z_window(way, at, c):
                x.start()
        for way in (0, 1):
            for x in z_window(way, at, c):
                x.wait_recv()
        half(c)
        at = pl.ds(pl.multiple_of(8 * c + 8, 8), 8)
        for way in (0, 1):
            h_window(way, at, c).start()
        for way in (0, 1):
            h_window(way, at, c).wait_recv()
        full(c)

        @pl.when(c == 2)
        def _():
            send_out(*first_at)
            send_out(*body_at(1))

        @pl.when(c >= 2)
        def _():
            send_out(*body_at(c))

        for at_step, hop, slot in ((4, 1, 0), (5, 2, 1)):

            @pl.when(c == at_step)
            def _():
                for n in (hop, nz - hop):
                    pl.semaphore_signal(
                        tok.at[slot], inc=1, device_id={"gz": lax.rem(gz + n, nz)},
                        device_id_type=MESH,
                    )

            @pl.when(c == at_step + 1)
            def _():
                pl.semaphore_wait(tok.at[slot], 2)

        return 0

    lax.fori_loop(0, tiles - 1, step, 0)

    last = tiles - 1
    wait_edges(1)
    wait_tile(last)
    ends = ((pl.ds(8 * last + 7, 8), last), (pl.ds(8 * tiles + 7, 2), tiles))
    for at, c in ends:
        for way in (0, 1):
            for x in z_window(way, at, c):
                x.start()
    for at, c in ends:
        for way in (0, 1):
            for x in z_window(way, at, c):
                x.wait_recv()
    half(last)
    half(tiles)
    ends = ((pl.ds(8 * last + 8, 8), last), (pl.ds(8 * tiles + 8, 1), tiles))
    for at, c in ends:
        for way in (0, 1):
            h_window(way, at, c).start()
    for at, c in ends:
        for way in (0, 1):
            h_window(way, at, c).wait_recv()
    full(last)
    full(tiles)
    send_out(*body_at(last))
    send_out(pl.ds(8 * tiles, 2), pl.ds(rows - 2, 2))

    def meet(own, box, axis, size, me, send, recv):
        for d in range(1, size):
            copy(own, box.at[me], send.at[d], recv.at[d], {axis: lax.rem(me + d, size)}).start()
        for d in range(1, size):
            copy(own, box.at[me], send.at[d], recv.at[d], {axis: lax.rem(me + d, size)}).wait()

    part = jnp.sum(acc[...], axis=1)
    part = jnp.concatenate([part, jnp.zeros_like(part)], 0)
    SM[0] = part
    SA[gx] = part
    meet(SM.at[0], SA, "gx", nx, gx, sa_s, sa_r)
    part = SA[0]
    for i in range(1, nx):
        part = part + SA[i]
    SM[1] = part
    SB[gy] = part
    meet(SM.at[1], SB, "gy", ny, gy, sb_s, sb_r)
    planes = SB[...]
    total = jnp.sum(planes, axis=0)
    SM[2] = total
    SC[gz] = total
    meet(SM.at[2], SC, "gz", nz, gz, sc_s, sc_r)
    offset = jnp.zeros_like(total)
    for i in range(nz):
        offset = offset + jnp.where(i < gz, SC[i], 0.0)
    cells = 1.0 / (rows * nx * 128 * ny)
    run = jnp.sum(offset, axis=(0, 1), keepdims=True) * cells
    row = lax.broadcasted_iota(jnp.int32, (8, 128), 0)
    for g in range(ny):
        mean = jnp.broadcast_to(jnp.sum(planes[g], axis=1, keepdims=True) * cells, (8, 128))
        pm_ref[g] = mean
        upto = mean + jnp.where(row >= 1, pltpu.roll(mean, 1, 0), 0.0)
        upto = upto + jnp.where(row >= 2, pltpu.roll(upto, 2, 0), 0.0)
        rank = (row + (gz * 4 * ny + 4 * g + 1)).astype(jnp.float32)
        rm_ref[g] = (run + upto) / rank
        run = run + upto[3:4, 0:1]

    for d in range(ny):
        whole = o_ref.at[pl.ds(0, 4)]
        if d == 0:
            pltpu.make_async_copy(N.at[:, 0, pl.ds(0, rows), :], whole, orem.at[0]).wait()
        else:
            end = copy(
                N.at[:, 0, pl.ds(0, rows), :], whole, osem.at[d], orem.at[d],
                {"gy": lax.rem(gy + d, ny)},
            )
            end.wait()
    for d in range(1, nx):
        to = {"gx": lax.rem(gx + d, nx)}
        at = pl.ds(8, rows)
        copy(E.at[1, :, at, :], E.at[1, :, at, :], xsE.at[d], xrE.at[d, 0], to).wait_send()
        copy(F.at[:, 1, :, at, :], F.at[:, 1, :, at, :], xsF.at[d], xrF.at[d, 0], to).wait_send()
        for side in (0, 1):

            @pl.when(has_edge(lax.rem(gx + d, nx), side))
            def _():
                for x in x_edge(d, side):
                    x.wait_send()
    for way in (0, 1):
        for x in z_window(way, pl.ds(7, rows + 2), 0):
            x.wait_send()
        h_window(way, pl.ds(8, rows + 1), 0).wait_send()


def per_device(energy, flow):
    nx, ny, nz = (lax.axis_size(a) for a in ("gx", "gy", "gz"))
    e = energy.reshape(32, 8, 8, 128).transpose(0, 2, 1, 3)
    f = flow.reshape(4, 32, 8, 8, 128).transpose(0, 1, 3, 2, 4)
    vmem = pl.BlockSpec(memory_space=pltpu.VMEM)
    hbm = pl.BlockSpec(memory_space=pl.ANY)
    f32 = jnp.float32
    dma = pltpu.SemaphoreType.DMA
    result, mean, running = pl.pallas_call(
        functools.partial(kernel, nx, ny, nz),
        out_shape=(
            jax.ShapeDtypeStruct((32, 64, 128), f32),
            jax.ShapeDtypeStruct((8, 8, 128), f32),
            jax.ShapeDtypeStruct((8, 8, 128), f32),
        ),
        in_specs=[hbm, hbm],
        out_specs=(hbm, vmem, vmem),
        scratch_shapes=[
            pltpu.VMEM((6, 8, 88, 128), f32),
            pltpu.VMEM((4, 6, 8, 88, 128), f32),
            pltpu.VMEM((6, 8, 88, 128), f32),
            pltpu.VMEM((4, 8, 72, 128), f32),
            pltpu.VMEM((4, 8, 128), f32),
            pltpu.VMEM((4, 8, 128), f32),
            pltpu.VMEM((8, 8, 128), f32),
            pltpu.VMEM((8, 8, 128), f32),
            pltpu.VMEM((3, 8, 128), f32),
            dma((4,)), dma((4,)), dma((4, 8)), dma((4, 8)),
            dma((4, 2)), dma((4, 2)), dma((4, 2)), dma((4, 2)), dma((4, 2)), dma((4, 2)),
            dma((2,)), dma((2,)), dma((2,)), dma((2, 9)), dma((2, 9)), dma((2, 9)),
            dma((8,)), dma((8,)),
            dma((4,)), dma((4,)), dma((8,)), dma((8,)), dma((8,)), dma((8,)),
            pltpu.SemaphoreType.REGULAR((2,)),
        ],
        compiler_params=pltpu.CompilerParams(collective_id=0, has_side_effects=True),
        name="two_steps",
    )(e, f)
    return result, mean[:, :4, 0].reshape(-1), running[:, :4, 0].reshape(-1)


def solution(mesh):
    placed = (P(("gz", "gy", "gx"), None, None), P(None, ("gz", "gy", "gx"), None, None))
    return jax.shard_map(
        per_device,
        mesh=mesh,
        in_specs=placed,
        out_specs=(P("gz", "gx", "gy"), P("gz"), P("gz")),
        check_vma=False,
    )
```

time: 286 us -> 118 us (0.41)
  the two profiles are of different devices: /device:TPU:24 before, /device:TPU:1 now
where the time goes in v1:
time: 118 us
  Pallas kernels  113 us (96%)
  local copies, waits for them, and re-layouts  4.35 us (4%)
    pallas_call x1, Pallas kernels, per_device(): pl.pallas_call(functools.partial(kernel, nx, ny, nz), out_shape=(jax.Shap...  113 us

profile of v1, /device:TPU:1, one launch (start us, length us, event | category | flops | bytes accessed | tf_op | source)
XLA Modules:
  0.0 118.2 jit_solution(10196164700694221306)
XLA Ops:
  0.6 113.2 %two_steps.1 = (f32[32,64,128]{2,1,0:T(8,128)}, f32[8,8,128]{2,1,0:T(8,128)}, f32[8,8,128]{2,1,0:T(8,128)}) custom-call(f32[32,8,8,128]{3,2,1,0:T(8,128)} %bitcast.7, f32[4,32,8,8,128]{4,3,2,1,0:T(8,128)} %bitcast.6), custom_call_target="tpu_custom_call" | custom-call | tf_op jit(solution)/shard_map/two_steps/pallas_call | solution.py:370
  113.9 0.9 slice_reduce_fusion
  114.7 0.6 reshape_squeeze.6
  115.3 0.6 reshape_squeeze.7
  115.9 2.3 %copy.6 = f32[32,64,128]{2,1,0:T(8,128)} copy(f32[32,64,128]{2,1,0:T(8,128)} %get-tuple-element.14) | data formatting | bytes 2097152

commit v2 on v1

--- a/solution.py
+++ b/solution.py
@@ -63,6 +63,7 @@
     m = gz * ny + gy
     up, down = lax.rem(m + 1, ring), lax.rem(m + ring - 1, ring)
     chain = tuple({"gy": lax.rem(n, ny), "gz": n // ny} for n in (up, down))
+    rounds = (ring - 1).bit_length() - 1
     rows = 64
     tiles = rows // 8
 
@@ -221,75 +222,103 @@
         start_tile(c)
     wait_edges(0)
 
-    def step(c, _):
-        @pl.when(c + AHEAD < tiles)
-        def _():
-            start_tile(c + AHEAD)
-
-        wait_tile(c)
-        at = pl.ds(8 * c + 7, 8)
+    def greet(r):
+        for n in (2**r, ring - 2**r):
+            to = lax.rem(m + n, ring)
+            pl.semaphore_signal(
+                tok.at[r], inc=1, device_id={"gy": lax.rem(to, ny), "gz": to // ny},
+                device_id_type=MESH,
+            )
+
+    def start_z(at, c):
         for way in (0, 1):
             for x in z_window(way, at, c):
                 x.start()
+
+    def wait_z(at, c):
         for way in (0, 1):
             for x in z_window(way, at, c):
                 x.wait_recv()
-        half(c)
-        at = pl.ds(pl.multiple_of(8 * c + 8, 8), 8)
+
+    def start_h(at, c):
         for way in (0, 1):
             h_window(way, at, c).start()
+
+    def wait_h(at, c):
         for way in (0, 1):
             h_window(way, at, c).wait_recv()
-        full(c)
-
-        @pl.when(c == 2)
+
+    def z_at(c):
+        return pl.ds(8 * c + 7, 8)
+
+    def h_at(c):
+        return pl.ds(pl.multiple_of(8 * c + 8, 8), 8)
+
+    z_end, h_end = pl.ds(8 * tiles + 7, 2), pl.ds(8 * tiles + 8, 1)
+    last = tiles - 1
+
+    def step(c, _):
+        @pl.when(c + AHEAD < tiles)
+        def _():
+            start_tile(c + AHEAD)
+
+        for r in range(rounds):
+
+            @pl.when(c == r)
+            def _():
+                if r > 0:
+                    pl.semaphore_wait(tok.at[r - 1], 2)
+                greet(r)
+
+        @pl.when(c == rounds)
+        def _():
+            pl.semaphore_wait(tok.at[rounds - 1], 2)
+
+        @pl.when(c == last)
+        def _():
+            wait_edges(1)
+
+        wait_tile(c)
+        start_z(z_at(c), c)
+
+        @pl.when(c == last)
+        def _():
+            start_z(z_end, tiles)
+
+        @pl.when(c >= 1)
+        def _():
+            wait_z(z_at(c - 1), c - 1)
+            half(c - 1)
+            start_h(h_at(c - 1), c - 1)
+
+        @pl.when(c >= 2)
+        def _():
+            wait_h(h_at(c - 2), c - 2)
+            full(c - 2)
+
+        @pl.when(c == 4)
         def _():
             send_out(*first_at)
             send_out(*body_at(1))
 
-        @pl.when(c >= 2)
-        def _():
-            send_out(*body_at(c))
-
-        for at_step, hop, slot in ((4, 1, 0), (5, 2, 1)):
-
-            @pl.when(c == at_step)
-            def _():
-                for n in (hop, nz - hop):
-                    pl.semaphore_signal(
-                        tok.at[slot], inc=1, device_id={"gz": lax.rem(gz + n, nz)},
-                        device_id_type=MESH,
-                    )
-
-            @pl.when(c == at_step + 1)
-            def _():
-                pl.semaphore_wait(tok.at[slot], 2)
+        @pl.when(c >= 4)
+        def _():
+            send_out(*body_at(c - 2))
 
         return 0
 
-    lax.fori_loop(0, tiles - 1, step, 0)
-
-    last = tiles - 1
-    wait_edges(1)
-    wait_tile(last)
-    ends = ((pl.ds(8 * last + 7, 8), last), (pl.ds(8 * tiles + 7, 2), tiles))
-    for at, c in ends:
-        for way in (0, 1):
-            for x in z_window(way, at, c):
-                x.start()
-    for at, c in ends:
-        for way in (0, 1):
-            for x in z_window(way, at, c):
-                x.wait_recv()
+    lax.fori_loop(0, tiles, step, 0)
+    wait_z(z_at(last), last)
+    wait_z(z_end, tiles)
     half(last)
     half(tiles)
-    ends = ((pl.ds(8 * last + 8, 8), last), (pl.ds(8 * tiles + 8, 1), tiles))
-    for at, c in ends:
-        for way in (0, 1):
-            h_window(way, at, c).start()
-    for at, c in ends:
-        for way in (0, 1):
-            h_window(way, at, c).wait_recv()
+    start_h(h_at(last), last)
+    start_h(h_end, tiles)
+    wait_h(h_at(last - 1), last - 1)
+    full(last - 1)
+    send_out(*body_at(last - 1))
+    wait_h(h_at(last), last)
+    wait_h(h_end, tiles)
     full(last)
     full(tiles)
     send_out(*body_at(last))
@@ -391,7 +420,7 @@
             dma((2,)), dma((2,)), dma((2,)), dma((2, 9)), dma((2, 9)), dma((2, 9)),
             dma((8,)), dma((8,)),
             dma((4,)), dma((4,)), dma((8,)), dma((8,)), dma((8,)), dma((8,)),
-            pltpu.SemaphoreType.REGULAR((2,)),
+            pltpu.SemaphoreType.REGULAR((8,)),
         ],
         compiler_params=pltpu.CompilerParams(collective_id=0, has_side_effects=True),
         name="two_steps",

time: 118 us -> 99.7 us (0.84)
  Pallas kernels: 113 us -> 94.5 us
    pallas_call x1, Pallas kernels: 113 us -> 94.5 us  [per_device(): pl.pallas_call(functools.partial(kernel, nx, ny, nz), out_shape=(jax.Shap...]
where the time goes in v2:
time: 99.7 us; the launch traced here: 99.5 us
  Pallas kernels  94.5 us (95%)
  local copies, waits for them, and re-layouts  4.35 us (4%)
    pallas_call x1, Pallas kernels, per_device(): pl.pallas_call(functools.partial(kernel, nx, ny, nz), out_shape=(jax.Shap...  94.5 us
    unnamed x1, local copies, waits for them, and re-layouts  2.31 us

profile of v2, /device:TPU:1, one launch (start us, length us, event | category | flops | bytes accessed | tf_op | source)
XLA Modules:
  0.0 99.5 jit_solution(130593729466836999)
XLA Ops:
  0.6 94.5 %two_steps.1 = (f32[32,64,128]{2,1,0:T(8,128)}, f32[8,8,128]{2,1,0:T(8,128)}, f32[8,8,128]{2,1,0:T(8,128)}) custom-call(f32[32,8,8,128]{3,2,1,0:T(8,128)} %bitcast.7, f32[4,32,8,8,128]{4,3,2,1,0:T(8,128)} %bitcast.6), custom_call_target="tpu_custom_call" | custom-call | tf_op jit(solution)/shard_map/two_steps/pallas_call | solution.py:399
  95.1 0.9 slice_reduce_fusion
  96.0 0.6 reshape_squeeze.6
  96.6 0.6 reshape_squeeze.7
  97.2 2.3 %copy.6 = f32[32,64,128]{2,1,0:T(8,128)} copy(f32[32,64,128]{2,1,0:T(8,128)} %get-tuple-element.14) | data formatting | bytes 2097152

commit v3 on v2

--- a/solution.py
+++ b/solution.py
@@ -54,9 +54,9 @@
 
 
 def kernel(
-    nx, ny, nz, e_ref, f_ref, o_ref, pm_ref, rm_ref, E, F, H, N, acc, SA, SB, SC, SM,
+    nx, ny, nz, e_ref, f_ref, o_ref, pm_ref, rm_ref, E, F, H, N, acc, SA, SC, SM,
     xsE, xsF, xrE, xrF, gsE, gsK, gsU, grE, grK, grU, zsE, zsK, zsH, zrE, zrK, zrH,
-    osem, orem, sa_s, sa_r, sb_s, sb_r, sc_s, sc_r, tok,
+    osem, orem, sa_s, sa_r, sc_s, sc_r, tok,
 ):
     gx, gy, gz = (lax.axis_index(a) for a in ("gx", "gy", "gz"))
     ring = ny * nz
@@ -321,45 +321,70 @@
     wait_h(h_end, tiles)
     full(last)
     full(tiles)
+
+    lane = lax.broadcasted_iota(jnp.int32, (1, 128), 1)
+    part = jnp.zeros((1, 128), jnp.float32)
+    for p in range(4):
+        part = part + jnp.where(
+            lane == 4 * gy + p, jnp.sum(acc[p], axis=(0, 1), keepdims=True), 0.0
+        )
+    SM[0] = part
+    SA[gx * ny + gy] = part
+
+    def group_row(n):
+        to = lax.rem(gx * ny + gy + n, nx * ny)
+        return copy(
+            SM.at[0], SA.at[gx * ny + gy], sa_s.at[n], sa_r.at[n],
+            {"gx": to // ny, "gy": lax.rem(to, ny)},
+        )
+
+    def start_row(n, _):
+        group_row(n).start()
+        return 0
+
+    def wait_row(n, _):
+        group_row(n).wait()
+        return 0
+
+    lax.fori_loop(1, nx * ny, start_row, 0)
     send_out(*body_at(last))
     send_out(pl.ds(8 * tiles, 2), pl.ds(rows - 2, 2))
-
-    def meet(own, box, axis, size, me, send, recv):
-        for d in range(1, size):
-            copy(own, box.at[me], send.at[d], recv.at[d], {axis: lax.rem(me + d, size)}).start()
-        for d in range(1, size):
-            copy(own, box.at[me], send.at[d], recv.at[d], {axis: lax.rem(me + d, size)}).wait()
-
-    part = jnp.sum(acc[...], axis=1)
-    part = jnp.concatenate([part, jnp.zeros_like(part)], 0)
-    SM[0] = part
-    SA[gx] = part
-    meet(SM.at[0], SA, "gx", nx, gx, sa_s, sa_r)
-    part = SA[0]
-    for i in range(1, nx):
-        part = part + SA[i]
-    SM[1] = part
-    SB[gy] = part
-    meet(SM.at[1], SB, "gy", ny, gy, sb_s, sb_r)
-    planes = SB[...]
-    total = jnp.sum(planes, axis=0)
-    SM[2] = total
-    SC[gz] = total
-    meet(SM.at[2], SC, "gz", nz, gz, sc_s, sc_r)
-    offset = jnp.zeros_like(total)
-    for i in range(nz):
-        offset = offset + jnp.where(i < gz, SC[i], 0.0)
+    lax.fori_loop(1, nx * ny, wait_row, 0)
+    planes = jnp.sum(SA[...], axis=0)
+    SM[1] = planes
+
+    def lift(d):
+        return copy(SM.at[1], SC.at[gz], sc_s.at[d], sc_r.at[d], {"gz": lax.rem(gz + d, nz)})
+
+    for d in range(1, nz):
+
+        @pl.when(gz + d < nz)
+        def _():
+            lift(d).start()
+
+    for d in range(1, nz):
+
+        @pl.when(gz >= d)
+        def _():
+            lift(d).wait_recv()
+
+    below = jnp.zeros_like(planes)
+    for n in range(nz - 1):
+        below = below + jnp.where(n < gz, SC[n], 0.0)
     cells = 1.0 / (rows * nx * 128 * ny)
-    run = jnp.sum(offset, axis=(0, 1), keepdims=True) * cells
-    row = lax.broadcasted_iota(jnp.int32, (8, 128), 0)
-    for g in range(ny):
-        mean = jnp.broadcast_to(jnp.sum(planes[g], axis=1, keepdims=True) * cells, (8, 128))
-        pm_ref[g] = mean
-        upto = mean + jnp.where(row >= 1, pltpu.roll(mean, 1, 0), 0.0)
-        upto = upto + jnp.where(row >= 2, pltpu.roll(upto, 2, 0), 0.0)
-        rank = (row + (gz * 4 * ny + 4 * g + 1)).astype(jnp.float32)
-        rm_ref[g] = (run + upto) / rank
-        run = run + upto[3:4, 0:1]
+    mean = jnp.broadcast_to(planes * cells, (8, 128))
+    lane = lax.broadcasted_iota(jnp.int32, (8, 128), 1)
+    upto = mean
+    for n in (1, 2, 4, 8, 16):
+        upto = upto + jnp.where(lane >= n, pltpu.roll(upto, n, 1), 0.0)
+    rank = (lane + (gz * 4 * ny + 1)).astype(jnp.float32)
+    pm_ref[...] = mean
+    rm_ref[...] = (upto + jnp.sum(below, axis=(0, 1), keepdims=True) * cells) / rank
+    for d in range(1, nz):
+
+        @pl.when(gz + d < nz)
+        def _():
+            lift(d).wait_send()
 
     for d in range(ny):
         whole = o_ref.at[pl.ds(0, 4)]
@@ -400,8 +425,8 @@
         functools.partial(kernel, nx, ny, nz),
         out_shape=(
             jax.ShapeDtypeStruct((32, 64, 128), f32),
-            jax.ShapeDtypeStruct((8, 8, 128), f32),
-            jax.ShapeDtypeStruct((8, 8, 128), f32),
+            jax.ShapeDtypeStruct((8, 128), f32),
+            jax.ShapeDtypeStruct((8, 128), f32),
         ),
         in_specs=[hbm, hbm],
         out_specs=(hbm, vmem, vmem),
@@ -411,21 +436,20 @@
             pltpu.VMEM((6, 8, 88, 128), f32),
             pltpu.VMEM((4, 8, 72, 128), f32),
             pltpu.VMEM((4, 8, 128), f32),
-            pltpu.VMEM((4, 8, 128), f32),
-            pltpu.VMEM((8, 8, 128), f32),
-            pltpu.VMEM((8, 8, 128), f32),
-            pltpu.VMEM((3, 8, 128), f32),
+            pltpu.VMEM((32, 1, 128), f32),
+            pltpu.VMEM((8, 1, 128), f32),
+            pltpu.VMEM((2, 1, 128), f32),
             dma((4,)), dma((4,)), dma((4, 8)), dma((4, 8)),
             dma((4, 2)), dma((4, 2)), dma((4, 2)), dma((4, 2)), dma((4, 2)), dma((4, 2)),
             dma((2,)), dma((2,)), dma((2,)), dma((2, 9)), dma((2, 9)), dma((2, 9)),
             dma((8,)), dma((8,)),
-            dma((4,)), dma((4,)), dma((8,)), dma((8,)), dma((8,)), dma((8,)),
+            dma((32,)), dma((32,)), dma((8,)), dma((8,)),
             pltpu.SemaphoreType.REGULAR((8,)),
         ],
         compiler_params=pltpu.CompilerParams(collective_id=0, has_side_effects=True),
         name="two_steps",
     )(e, f)
-    return result, mean[:, :4, 0].reshape(-1), running[:, :4, 0].reshape(-1)
+    return result, mean[0, :32], running[0, :32]
 
 
 def solution(mesh):

time: 99.7 us -> 95 us (0.953)
  the two profiles are of different devices: /device:TPU:1 before, /device:TPU:24 now
where the time goes in v3:
time: 95 us; the launch traced here: 94.9 us
  Pallas kernels  90.7 us (95%)
  local copies, waits for them, and re-layouts  3.5 us (4%)
    pallas_call x1, Pallas kernels, per_device(): pl.pallas_call(functools.partial(kernel, nx, ny, nz), out_shape=(jax.Shap...  90.7 us
    unnamed x1, local copies, waits for them, and re-layouts  2.31 us

profile of v3, /device:TPU:24, one launch (start us, length us, event | category | flops | bytes accessed | tf_op | source)
XLA Modules:
  0.0 94.9 jit_solution(16179344159273338907)
XLA Ops:
  0.6 90.7 %two_steps.1 = (f32[32,64,128]{2,1,0:T(8,128)}, f32[8,128]{1,0:T(8,128)}, f32[8,128]{1,0:T(8,128)}) custom-call(f32[32,8,8,128]{3,2,1,0:T(8,128)} %bitcast.11, f32[4,32,8,8,128]{4,3,2,1,0:T(8,128)} %bitcast.10), custom_call_target="tpu_custom_call" | custom-call | tf_op jit(solution)/shard_map/two_steps/pallas_call | solution.py:424
  91.3 1.2 %slice_bitcast_fusion = (f32[32]{0:T(128)}, f32[32]{0:T(128)}) fusion(f32[8,128]{1,0:T(8,128)} %get-tuple-element.8, f32[8,128]{1,0:T(8,128)} %get-tuple-element.7), kind=kLoop, calls=%fused_computation | loop fusion | bytes 512 | tf_op jit(solution)/shard_map/squeeze | solution.py:452
  92.5 2.3 %copy.6 = f32[32,64,128]{2,1,0:T(8,128)} copy(f32[32,64,128]{2,1,0:T(8,128)} %get-tuple-element.14) | data formatting | bytes 2097152

commit v4 on v3

--- a/solution.py
+++ b/solution.py
@@ -81,20 +81,17 @@
             device_id_type=MESH,
         )
 
-    def x_tile(d, c):
+    def x_rows(d, part, c):
         t = lax.rem(gx + d, nx)
-        src = (e_ref.at[t * tiles + c], f_ref.at[:, t * tiles + c])
-        at = pl.ds(pl.multiple_of(8 + 8 * c, 8), 8)
-        dst = (E.at[1 + gx, :, at, :], F.at[:, 1 + gx, :, at, :])
+        inside = (pl.ds(0, 2), pl.ds(2, 6))[part]
+        at = pl.ds(8 + 8 * c + 2 * part, (2, 6)[part])
+        parts = (
+            (e_ref.at[t * tiles + c, :, inside, :], E.at[1 + gx, :, at, :], xsE, xrE),
+            (f_ref.at[:, t * tiles + c, :, inside, :], F.at[:, 1 + gx, :, at, :], xsF, xrF),
+        )
         if d == 0:
-            return (
-                pltpu.make_async_copy(src[0], dst[0], xrE.at[0, c]),
-                pltpu.make_async_copy(src[1], dst[1], xrF.at[0, c]),
-            )
-        return (
-            copy(src[0], dst[0], xsE.at[d], xrE.at[d, c], {"gx": t}),
-            copy(src[1], dst[1], xsF.at[d], xrF.at[d, c], {"gx": t}),
-        )
+            return [pltpu.make_async_copy(a, b, r.at[part, 0, c]) for a, b, s, r in parts]
+        return [copy(a, b, s.at[d], r.at[part, d, c], {"gx": t}) for a, b, s, r in parts]
 
     def x_edge(d, side):
         t = lax.rem(gx + d, nx)
@@ -122,10 +119,17 @@
     def has_edge(g, side):
         return g > 0 if side == 0 else g < nx - 1
 
+    def start_rows(part, c):
+        for d in range(nx):
+            for x in x_rows(d, part, c):
+                x.start()
+
     def start_tile(c):
-        for d in (0, *range(1, nx)):
-            for x in x_tile(d, c):
-                x.start()
+        start_rows(1, c)
+
+        @pl.when(c < tiles - 1)
+        def _():
+            start_rows(0, lax.min(c + 1, tiles - 1))
 
     def start_edges(side):
         for d in range(nx):
@@ -151,48 +155,61 @@
             H.at[src, :, at, :], H.at[dst, :, at, :], zsH.at[way], zrH.at[way, c], chain[way]
         )
 
-    def out_window(d, src_at, dst_at):
+    def out_window(d, at):
         t = lax.rem(gy + d, ny)
         return copy(
-            N.at[:, t, src_at, :], o_ref.at[pl.ds(4 * gy, 4), dst_at, :], osem.at[d], orem.at[d],
+            N.at[:, t, at, :], o_ref.at[pl.ds(4 * gy, 4), at, :], osem.at[d], orem.at[d],
             {"gy": t},
         )
 
-    def send_out(src_at, dst_at):
+    def send_out(at):
         def one(d, _):
-            out_window(d, src_at, dst_at).start()
+            out_window(d, at).start()
             return 0
 
         lax.fori_loop(1, ny, one, 0)
         pltpu.make_async_copy(
-            N.at[:, gy, src_at, :], o_ref.at[pl.ds(4 * gy, 4), dst_at, :], orem.at[0]
+            N.at[:, gy, at, :], o_ref.at[pl.ds(4 * gy, 4), at, :], orem.at[0]
         ).start()
 
-    def half(c):
-        def plane(p, _):
-            v = change_of(E, p, 8 * c + 7, F, 8 * c + 7)
-            r = lax.broadcasted_iota(jnp.int32, v.shape, 1) + (8 * c - 1 + rows * gx)
+    def over(planes, work):
+        def one(n, _):
+            work(planes[0] + (planes[1] - planes[0]) * n)
+            return 0
+
+        lax.fori_loop(0, 2, one, 0)
+
+    inner, outer = (2, 3), (1, 4)
+
+    def half(c, planes):
+        def plane(p):
+            v = change_of(E, p, 8 * c + 9, F, 8 * c + 9)
+            r = lax.broadcasted_iota(jnp.int32, v.shape, 1) + (8 * c + 1 + rows * gx)
             H[p, :, pl.ds(pl.multiple_of(8 * c + 8, 8), 8), :] = jnp.where(
                 (r >= 0) & (r < rows * nx), v, 0.0
             )
-            return 0
-
-        lax.fori_loop(1, 5, plane, 0)
-
-    def full(c):
-        def plane(p, _):
-            v = change_of(H, p, 8 * c + 7, F, 8 * c + 6)
+
+        over(planes, plane)
+
+    def full(c, planes):
+        def plane(p):
+            v = change_of(H, p, 8 * c + 7, F, pl.multiple_of(8 * c + 8, 8))
             N[p - 1, :, pl.ds(pl.multiple_of(8 * c, 8), 8), :] = v
-            r = lax.broadcasted_iota(jnp.int32, v.shape, 1) + (8 * c - 2)
-            acc[p - 1] += jnp.sum(jnp.where((r >= 0) & (r < rows), v, 0.0), axis=0)
-            return 0
-
-        lax.fori_loop(1, 5, plane, 0)
+            acc[p - 1] += jnp.sum(v, axis=0)
+
+        over(planes, plane)
+
+    def wait_rows(part, c):
+        for d in range(nx):
+            for x in x_rows(d, part, c):
+                x.wait() if d == 0 else x.wait_recv()
 
     def wait_tile(c):
-        for d in range(nx):
-            for x in x_tile(d, c):
-                x.wait() if d == 0 else x.wait_recv()
+        wait_rows(1, c)
+
+        @pl.when(c < tiles - 1)
+        def _():
+            wait_rows(0, lax.min(c + 1, tiles - 1))
 
     def wait_edges(side):
         @pl.when(has_edge(gx, side))
@@ -201,10 +218,8 @@
                 for x in x_edge(d, side):
                     x.wait() if d == 0 else x.wait_recv()
 
-    def body_at(c):
-        return pl.ds(pl.multiple_of(8 * c, 8), 8), pl.ds(8 * c - 2, 8)
-
-    first_at = (pl.ds(2, 6), pl.ds(0, 6))
+    def out_at(c):
+        return pl.ds(pl.multiple_of(8 * c, 8), 8)
 
     acc[...] = jnp.zeros_like(acc)
     for side, at in ((0, slice(6, 8)), (1, slice(8 + rows, 10 + rows))):
@@ -216,11 +231,13 @@
 
     pl.semaphore_wait(bar, nx + 1)
     start_edges(0)
+    start_rows(0, 0)
     start_tile(0)
     start_edges(1)
     for c in range(1, AHEAD):
         start_tile(c)
     wait_edges(0)
+    wait_rows(0, 0)
 
     def greet(r):
         for n in (2**r, ring - 2**r):
@@ -249,13 +266,14 @@
             h_window(way, at, c).wait_recv()
 
     def z_at(c):
-        return pl.ds(8 * c + 7, 8)
+        return pl.ds(8 * c + 9, 8)
 
     def h_at(c):
         return pl.ds(pl.multiple_of(8 * c + 8, 8), 8)
 
-    z_end, h_end = pl.ds(8 * tiles + 7, 2), pl.ds(8 * tiles + 8, 1)
+    z_first, h_first = pl.ds(7, 2), pl.ds(7, 1)
     last = tiles - 1
+    start_z(z_first, tiles)
 
     def step(c, _):
         @pl.when(c + AHEAD < tiles)
@@ -281,46 +299,53 @@
         wait_tile(c)
         start_z(z_at(c), c)
 
-        @pl.when(c == last)
-        def _():
-            start_z(z_end, tiles)
+        @pl.when(c == 1)
+        def _():
+            wait_z(z_first, tiles)
+            half(-1, inner)
+            half(-1, outer)
+            start_h(h_first, tiles)
 
         @pl.when(c >= 1)
         def _():
+            half(c - 1, inner)
             wait_z(z_at(c - 1), c - 1)
-            half(c - 1)
+            half(c - 1, outer)
             start_h(h_at(c - 1), c - 1)
 
+        @pl.when(c == 2)
+        def _():
+            wait_h(h_first, tiles)
+
         @pl.when(c >= 2)
         def _():
+            full(c - 2, inner)
             wait_h(h_at(c - 2), c - 2)
-            full(c - 2)
+            full(c - 2, outer)
 
         @pl.when(c == 4)
         def _():
-            send_out(*first_at)
-            send_out(*body_at(1))
+            send_out(out_at(0))
+            send_out(out_at(1))
 
         @pl.when(c >= 4)
         def _():
-            send_out(*body_at(c - 2))
+            send_out(out_at(c - 2))
 
         return 0
 
     lax.fori_loop(0, tiles, step, 0)
+    half(last, inner)
     wait_z(z_at(last), last)
-    wait_z(z_end, tiles)
-    half(last)
-    half(tiles)
+    half(last, outer)
     start_h(h_at(last), last)
-    start_h(h_end, tiles)
+    full(last - 1, inner)
     wait_h(h_at(last - 1), last - 1)
-    full(last - 1)
-    send_out(*body_at(last - 1))
+    full(last - 1, outer)
+    send_out(out_at(last - 1))
+    full(last, inner)
     wait_h(h_at(last), last)
-    wait_h(h_end, tiles)
-    full(last)
-    full(tiles)
+    full(last, outer)
 
     lane = lax.broadcasted_iota(jnp.int32, (1, 128), 1)
     part = jnp.zeros((1, 128), jnp.float32)
@@ -347,26 +372,37 @@
         return 0
 
     lax.fori_loop(1, nx * ny, start_row, 0)
-    send_out(*body_at(last))
-    send_out(pl.ds(8 * tiles, 2), pl.ds(rows - 2, 2))
+    send_out(out_at(last))
     lax.fori_loop(1, nx * ny, wait_row, 0)
     planes = jnp.sum(SA[...], axis=0)
     SM[1] = planes
 
-    def lift(d):
-        return copy(SM.at[1], SC.at[gz], sc_s.at[d], sc_r.at[d], {"gz": lax.rem(gz + d, nz)})
-
-    for d in range(1, nz):
-
-        @pl.when(gz + d < nz)
-        def _():
-            lift(d).start()
-
-    for d in range(1, nz):
-
-        @pl.when(gz >= d)
-        def _():
-            lift(d).wait_recv()
+    def lift(to_z, to_y, slot):
+        return copy(
+            SM.at[1], SC.at[gz], sc_s.at[to_z, slot], sc_r.at[gz], {"gy": to_y, "gz": to_z}
+        )
+
+    def lifts(act):
+        for to in range(1, nz):
+            alike = lax.rem(gz + to, 2) == 0
+
+            @pl.when((gz < to) & alike)
+            def _():
+                act(lift(to, gy, 0))
+
+            for end, first in ((ny - 1, 0), (1, ny // 2)):
+
+                @pl.when((gz < to) & jnp.logical_not(alike) & (gy == end))
+                def _():
+                    for n in range(ny // 2):
+                        act(lift(to, first + n, n))
+
+    lifts(lambda x: x.start())
+    for n in range(nz - 1):
+
+        @pl.when(n < gz)
+        def _():
+            copy(SM.at[1], SC.at[n], sc_s.at[0, 0], sc_r.at[n], {"gz": gz}).wait_recv()
 
     below = jnp.zeros_like(planes)
     for n in range(nz - 1):
@@ -380,11 +416,7 @@
     rank = (lane + (gz * 4 * ny + 1)).astype(jnp.float32)
     pm_ref[...] = mean
     rm_ref[...] = (upto + jnp.sum(below, axis=(0, 1), keepdims=True) * cells) / rank
-    for d in range(1, nz):
-
-        @pl.when(gz + d < nz)
-        def _():
-            lift(d).wait_send()
+    lifts(lambda x: x.wait_send())
 
     for d in range(ny):
         whole = o_ref.at[pl.ds(0, 4)]
@@ -399,8 +431,8 @@
     for d in range(1, nx):
         to = {"gx": lax.rem(gx + d, nx)}
         at = pl.ds(8, rows)
-        copy(E.at[1, :, at, :], E.at[1, :, at, :], xsE.at[d], xrE.at[d, 0], to).wait_send()
-        copy(F.at[:, 1, :, at, :], F.at[:, 1, :, at, :], xsF.at[d], xrF.at[d, 0], to).wait_send()
+        copy(E.at[1, :, at, :], E.at[1, :, at, :], xsE.at[d], xrE.at[0, d, 0], to).wait_send()
+        copy(F.at[:, 1, :, at, :], F.at[:, 1, :, at, :], xsF.at[d], xrF.at[0, d, 0], to).wait_send()
         for side in (0, 1):
 
             @pl.when(has_edge(lax.rem(gx + d, nx), side))
@@ -410,7 +442,7 @@
     for way in (0, 1):
         for x in z_window(way, pl.ds(7, rows + 2), 0):
             x.wait_send()
-        h_window(way, pl.ds(8, rows + 1), 0).wait_send()
+        h_window(way, pl.ds(7, rows + 1), 0).wait_send()
 
 
 def per_device(energy, flow):
@@ -431,22 +463,24 @@
         in_specs=[hbm, hbm],
         out_specs=(hbm, vmem, vmem),
         scratch_shapes=[
-            pltpu.VMEM((6, 8, 88, 128), f32),
-            pltpu.VMEM((4, 6, 8, 88, 128), f32),
-            pltpu.VMEM((6, 8, 88, 128), f32),
-            pltpu.VMEM((4, 8, 72, 128), f32),
+            pltpu.VMEM((6, 8, 80, 128), f32),
+            pltpu.VMEM((4, 6, 8, 80, 128), f32),
+            pltpu.VMEM((6, 8, 80, 128), f32),
+            pltpu.VMEM((4, 8, 64, 128), f32),
             pltpu.VMEM((4, 8, 128), f32),
             pltpu.VMEM((32, 1, 128), f32),
             pltpu.VMEM((8, 1, 128), f32),
             pltpu.VMEM((2, 1, 128), f32),
-            dma((4,)), dma((4,)), dma((4, 8)), dma((4, 8)),
+            dma((4,)), dma((4,)), dma((2, 4, 8)), dma((2, 4, 8)),
             dma((4, 2)), dma((4, 2)), dma((4, 2)), dma((4, 2)), dma((4, 2)), dma((4, 2)),
             dma((2,)), dma((2,)), dma((2,)), dma((2, 9)), dma((2, 9)), dma((2, 9)),
             dma((8,)), dma((8,)),
-            dma((32,)), dma((32,)), dma((8,)), dma((8,)),
+            dma((32,)), dma((32,)), dma((8, 4)), dma((8,)),
             pltpu.SemaphoreType.REGULAR((8,)),
         ],
-        compiler_params=pltpu.CompilerParams(collective_id=0, has_side_effects=True),
+        compiler_params=pltpu.CompilerParams(
+            collective_id=0, has_side_effects=True, vmem_limit_bytes=55_000_000
+        ),
         name="two_steps",
     )(e, f)
     return result, mean[0, :32], running[0, :32]

time: 95 us -> 90.2 us (0.949)
  Pallas kernels: 90.7 us -> 88 us
  local copies, waits for them, and re-layouts: 3.5 us -> 1.49 us
    pallas_call x1, Pallas kernels: 90.7 us -> 88 us  [per_device(): pl.pallas_call(functools.partial(kernel, nx, ny, nz), out_shape=(jax.Shap...]
    unnamed x1, local copies, waits for them, and re-layouts: 2.31 us -> 0.97 us
where the time goes in v4:
time: 90.2 us; the launch traced here: 90.1 us
  Pallas kernels  88 us (98%)
  local copies, waits for them, and re-layouts  1.49 us (2%)
    pallas_call x1, Pallas kernels, per_device(): pl.pallas_call(functools.partial(kernel, nx, ny, nz), out_shape=(jax.Shap...  88 us

profile of v4, /device:TPU:24, one launch (start us, length us, event | category | flops | bytes accessed | tf_op | source)
XLA Modules:
  0.0 90.1 jit_solution(11535765397800277308)
XLA Ops:
  0.6 88.0 %two_steps.1 = (f32[32,64,128]{2,1,0:T(8,128)S(1)}, f32[8,128]{1,0:T(8,128)S(1)}, f32[8,128]{1,0:T(8,128)S(1)}) custom-call(f32[32,8,8,128]{3,2,1,0:T(8,128)} %bitcast.11, f32[4,32,8,8,128]{4,3,2,1,0:T(8,128)} %bitcast.10), custom_call_target="tpu_custom_call" | custom-call | tf_op jit(solution)/shard_map/two_steps/pallas_call | solution.py:456
  88.6 0.5 slice_bitcast_fusion
  89.1 1.0 %copy.6 = f32[32,64,128]{2,1,0:T(8,128)} copy(f32[32,64,128]{2,1,0:T(8,128)S(1)} %get-tuple-element.14) | data formatting | bytes 2097152

commit v5 on v4

--- a/solution.py
+++ b/solution.py
@@ -55,7 +55,7 @@
 
 def kernel(
     nx, ny, nz, e_ref, f_ref, o_ref, pm_ref, rm_ref, E, F, H, N, acc, SA, SC, SM,
-    xsE, xsF, xrE, xrF, gsE, gsK, gsU, grE, grK, grU, zsE, zsK, zsH, zrE, zrK, zrH,
+    xsE, xsF, xrE, xrF, gsE, gsK, grE, grK, xsH, xrH, zsE, zsK, zsH, zrE, zrK, zrH,
     osem, orem, sa_s, sa_r, sc_s, sc_r, tok,
 ):
     gx, gy, gz = (lax.axis_index(a) for a in ("gx", "gy", "gz"))
@@ -96,25 +96,23 @@
     def x_edge(d, side):
         t = lax.rem(gx + d, nx)
         if side == 0:
-            tile = lax.max(t * tiles - 1, 0)
-            wide, narrow, wide_at, narrow_at = pl.ds(6, 2), pl.ds(7, 1), pl.ds(6, 2), pl.ds(7, 1)
+            tile, row, at = lax.max(t * tiles - 1, 0), pl.ds(7, 1), pl.ds(7, 1)
         else:
-            tile = lax.min((t + 1) * tiles, nx * tiles - 1)
-            wide, narrow = pl.ds(0, 2), pl.ds(0, 1)
-            wide_at, narrow_at = pl.ds(8 + rows, 2), pl.ds(8 + rows, 1)
+            tile, row, at = lax.min((t + 1) * tiles, nx * tiles - 1), pl.ds(0, 1), pl.ds(8 + rows, 1)
         parts = (
-            (e_ref.at[tile, :, wide, :], E.at[1 + gx, :, wide_at, :], gsE, grE),
-            (f_ref.at[3, tile, :, wide, :], F.at[3, 1 + gx, :, wide_at, :], gsK, grK),
-            (
-                f_ref.at[pl.ds(0, 3), tile, :, narrow, :],
-                F.at[pl.ds(0, 3), 1 + gx, :, narrow_at, :],
-                gsU,
-                grU,
-            ),
+            (e_ref.at[tile, :, row, :], E.at[1 + gx, :, at, :], gsE, grE),
+            (f_ref.at[3, tile, :, row, :], F.at[3, 1 + gx, :, at, :], gsK, grK),
         )
         if d == 0:
             return [pltpu.make_async_copy(a, b, r.at[0, side]) for a, b, s, r in parts]
         return [copy(a, b, s.at[d, side], r.at[d, side], {"gx": t}) for a, b, s, r in parts]
+
+    def x_half(side):
+        src, dst = ((7, 71), (70, 6))[side]
+        return copy(
+            H.at[pl.ds(1, 4), :, pl.ds(src, 1), :], H.at[pl.ds(1, 4), :, pl.ds(dst, 1), :],
+            xsH.at[side], xrH.at[side], {"gx": lax.rem(gx + (nx - 1, 1)[side], nx)},
+        )
 
     def has_edge(g, side):
         return g > 0 if side == 0 else g < nx - 1
@@ -181,13 +179,11 @@
 
     inner, outer = (2, 3), (1, 4)
 
-    def half(c, planes):
+    def half(c, planes, first=0, count=8):
         def plane(p):
             v = change_of(E, p, 8 * c + 9, F, 8 * c + 9)
-            r = lax.broadcasted_iota(jnp.int32, v.shape, 1) + (8 * c + 1 + rows * gx)
-            H[p, :, pl.ds(pl.multiple_of(8 * c + 8, 8), 8), :] = jnp.where(
-                (r >= 0) & (r < rows * nx), v, 0.0
-            )
+            at = 8 * c + 8 + first if count < 8 else pl.multiple_of(8 * c + 8, 8)
+            H[p, :, pl.ds(at, count), :] = v[:, first : first + count]
 
         over(planes, plane)
 
@@ -222,12 +218,14 @@
         return pl.ds(pl.multiple_of(8 * c, 8), 8)
 
     acc[...] = jnp.zeros_like(acc)
-    for side, at in ((0, slice(6, 8)), (1, slice(8 + rows, 10 + rows))):
+    for side, at, half_at in ((0, 7, 6), (1, 8 + rows, 7 + rows)):
 
         @pl.when(jnp.logical_not(has_edge(gx, side)))
         def _():
-            E[1:5, :, at, :] = jnp.zeros_like(E[1:5, :, at, :])
-            F[3, 1:5, :, at, :] = jnp.zeros_like(E[1:5, :, at, :])
+            none = jnp.zeros((4, ny, 1, 128), jnp.float32)
+            E[1:5, :, at : at + 1, :] = none
+            F[3, 1:5, :, at : at + 1, :] = none
+            H[1:5, :, half_at : half_at + 1, :] = none
 
     pl.semaphore_wait(bar, nx + 1)
     start_edges(0)
@@ -271,8 +269,9 @@
     def h_at(c):
         return pl.ds(pl.multiple_of(8 * c + 8, 8), 8)
 
-    z_first, h_first = pl.ds(7, 2), pl.ds(7, 1)
+    z_first, h_first = pl.ds(8, 1), pl.ds(7, 1)
     last = tiles - 1
+    h_last = pl.ds(8 * last + 8, 7)
     start_z(z_first, tiles)
 
     def step(c, _):
@@ -302,9 +301,13 @@
         @pl.when(c == 1)
         def _():
             wait_z(z_first, tiles)
-            half(-1, inner)
-            half(-1, outer)
+            half(-1, inner, 7, 1)
+            half(-1, outer, 7, 1)
             start_h(h_first, tiles)
+
+            @pl.when(has_edge(gx, 0))
+            def _():
+                x_half(0).start()
 
         @pl.when(c >= 1)
         def _():
@@ -317,7 +320,11 @@
         def _():
             wait_h(h_first, tiles)
 
-        @pl.when(c >= 2)
+        @pl.when(c == 2)
+        def _():
+            wait_h(h_at(0), 0)
+
+        @pl.when(c >= 3)
         def _():
             full(c - 2, inner)
             wait_h(h_at(c - 2), c - 2)
@@ -325,7 +332,6 @@
 
         @pl.when(c == 4)
         def _():
-            send_out(out_at(0))
             send_out(out_at(1))
 
         @pl.when(c >= 4)
@@ -335,17 +341,34 @@
         return 0
 
     lax.fori_loop(0, tiles, step, 0)
-    half(last, inner)
+    half(last, inner, 0, 7)
     wait_z(z_at(last), last)
-    half(last, outer)
-    start_h(h_at(last), last)
+    half(last, outer, 0, 7)
+    start_h(h_last, last)
+
+    @pl.when(has_edge(gx, 1))
+    def _():
+        x_half(1).start()
+
     full(last - 1, inner)
     wait_h(h_at(last - 1), last - 1)
     full(last - 1, outer)
     send_out(out_at(last - 1))
+
+    @pl.when(has_edge(gx, 1))
+    def _():
+        x_half(0).wait_recv()
+
     full(last, inner)
-    wait_h(h_at(last), last)
+    wait_h(h_last, last)
     full(last, outer)
+
+    @pl.when(has_edge(gx, 0))
+    def _():
+        x_half(1).wait_recv()
+
+    full(0, inner)
+    full(0, outer)
 
     lane = lax.broadcasted_iota(jnp.int32, (1, 128), 1)
     part = jnp.zeros((1, 128), jnp.float32)
@@ -373,6 +396,7 @@
 
     lax.fori_loop(1, nx * ny, start_row, 0)
     send_out(out_at(last))
+    send_out(out_at(0))
     lax.fori_loop(1, nx * ny, wait_row, 0)
     planes = jnp.sum(SA[...], axis=0)
     SM[1] = planes
@@ -439,10 +463,16 @@
             def _():
                 for x in x_edge(d, side):
                     x.wait_send()
+    for side in (0, 1):
+
+        @pl.when(has_edge(gx, side))
+        def _():
+            x_half(side).wait_send()
+
     for way in (0, 1):
-        for x in z_window(way, pl.ds(7, rows + 2), 0):
+        for x in z_window(way, pl.ds(8, rows + 1), 0):
             x.wait_send()
-        h_window(way, pl.ds(7, rows + 1), 0).wait_send()
+        h_window(way, pl.ds(7, rows), 0).wait_send()
 
 
 def per_device(energy, flow):
@@ -472,7 +502,7 @@
             pltpu.VMEM((8, 1, 128), f32),
             pltpu.VMEM((2, 1, 128), f32),
             dma((4,)), dma((4,)), dma((2, 4, 8)), dma((2, 4, 8)),
-            dma((4, 2)), dma((4, 2)), dma((4, 2)), dma((4, 2)), dma((4, 2)), dma((4, 2)),
+            dma((4, 2)), dma((4, 2)), dma((4, 2)), dma((4, 2)), dma((2,)), dma((2,)),
             dma((2,)), dma((2,)), dma((2,)), dma((2, 9)), dma((2, 9)), dma((2, 9)),
             dma((8,)), dma((8,)),
             dma((32,)), dma((32,)), dma((8, 4)), dma((8,)),

time: 90.2 us -> 89.2 us (0.989)
  Pallas kernels: 88 us -> 86.5 us
    pallas_call x1, Pallas kernels: 88 us -> 86.5 us  [per_device(): pl.pallas_call(functools.partial(kernel, nx, ny, nz), out_shape=(jax.Shap...]
where the time goes in v5:
time: 89.2 us; the launch traced here: 88.6 us
  Pallas kernels  86.5 us (97%)
  local copies, waits for them, and re-layouts  1.49 us (2%)
    pallas_call x1, Pallas kernels, per_device(): pl.pallas_call(functools.partial(kernel, nx, ny, nz), out_shape=(jax.Shap...  86.5 us

profile of v5, /device:TPU:24, one launch (start us, length us, event | category | flops | bytes accessed | tf_op | source)
XLA Modules:
  0.0 88.6 jit_solution(15985074347103223311)
XLA Ops:
  0.6 86.5 %two_steps.1 = (f32[32,64,128]{2,1,0:T(8,128)S(1)}, f32[8,128]{1,0:T(8,128)S(1)}, f32[8,128]{1,0:T(8,128)S(1)}) custom-call(f32[32,8,8,128]{3,2,1,0:T(8,128)} %bitcast.11, f32[4,32,8,8,128]{4,3,2,1,0:T(8,128)} %bitcast.10), custom_call_target="tpu_custom_call" | custom-call | tf_op jit(solution)/shard_map/two_steps/pallas_call | solution.py:486
  87.1 0.5 slice_bitcast_fusion
  87.6 1.0 %copy.6 = f32[32,64,128]{2,1,0:T(8,128)} copy(f32[32,64,128]{2,1,0:T(8,128)S(1)} %get-tuple-element.14) | data formatting | bytes 2097152

commit v6 on v5

--- a/solution.py
+++ b/solution.py
@@ -55,7 +55,7 @@
 
 def kernel(
     nx, ny, nz, e_ref, f_ref, o_ref, pm_ref, rm_ref, E, F, H, N, acc, SA, SC, SM,
-    xsE, xsF, xrE, xrF, gsE, gsK, grE, grK, xsH, xrH, zsE, zsK, zsH, zrE, zrK, zrH,
+    xsE, xsK, xsU, xrE, xrK, xrU, gsE, gsK, grE, grK, xsH, xrH, zsE, zsK, zsH, zrE, zrK, zrH,
     osem, orem, sa_s, sa_r, sc_s, sc_r, tok,
 ):
     gx, gy, gz = (lax.axis_index(a) for a in ("gx", "gy", "gz"))
@@ -81,14 +81,21 @@
             device_id_type=MESH,
         )
 
-    def x_rows(d, part, c):
+    def x_rows(kind, d, part, c):
         t = lax.rem(gx + d, nx)
         inside = (pl.ds(0, 2), pl.ds(2, 6))[part]
         at = pl.ds(8 + 8 * c + 2 * part, (2, 6)[part])
         parts = (
             (e_ref.at[t * tiles + c, :, inside, :], E.at[1 + gx, :, at, :], xsE, xrE),
-            (f_ref.at[:, t * tiles + c, :, inside, :], F.at[:, 1 + gx, :, at, :], xsF, xrF),
-        )
+            (f_ref.at[3, t * tiles + c, :, inside, :], F.at[3, 1 + gx, :, at, :], xsK, xrK),
+            (
+                f_ref.at[pl.ds(0, 3), t * tiles + c, :, inside, :],
+                F.at[pl.ds(0, 3), 1 + gx, :, at, :],
+                xsU,
+                xrU,
+            ),
+        )
+        parts = (parts[:2], parts[2:])[kind]
         if d == 0:
             return [pltpu.make_async_copy(a, b, r.at[part, 0, c]) for a, b, s, r in parts]
         return [copy(a, b, s.at[d], r.at[part, d, c], {"gx": t}) for a, b, s, r in parts]
@@ -117,17 +124,17 @@
     def has_edge(g, side):
         return g > 0 if side == 0 else g < nx - 1
 
-    def start_rows(part, c):
+    def start_rows(kind, part, c):
         for d in range(nx):
-            for x in x_rows(d, part, c):
+            for x in x_rows(kind, d, part, c):
                 x.start()
 
-    def start_tile(c):
-        start_rows(1, c)
+    def start_tile(kind, c):
+        start_rows(kind, 1, c)
 
         @pl.when(c < tiles - 1)
         def _():
-            start_rows(0, lax.min(c + 1, tiles - 1))
+            start_rows(kind, 0, lax.min(c + 1, tiles - 1))
 
     def start_edges(side):
         for d in range(nx):
@@ -195,17 +202,17 @@
 
         over(planes, plane)
 
-    def wait_rows(part, c):
+    def wait_rows(kind, part, c):
         for d in range(nx):
-            for x in x_rows(d, part, c):
+            for x in x_rows(kind, d, part, c):
                 x.wait() if d == 0 else x.wait_recv()
 
-    def wait_tile(c):
-        wait_rows(1, c)
+    def wait_tile(kind, c):
+        wait_rows(kind, 1, c)
 
         @pl.when(c < tiles - 1)
         def _():
-            wait_rows(0, lax.min(c + 1, tiles - 1))
+            wait_rows(kind, 0, lax.min(c + 1, tiles - 1))
 
     def wait_edges(side):
         @pl.when(has_edge(gx, side))
@@ -229,13 +236,15 @@
 
     pl.semaphore_wait(bar, nx + 1)
     start_edges(0)
-    start_rows(0, 0)
-    start_tile(0)
+    start_rows(0, 0, 0)
+    start_tile(0, 0)
     start_edges(1)
+    start_rows(1, 0, 0)
     for c in range(1, AHEAD):
-        start_tile(c)
+        start_tile(0, c)
+        start_tile(1, c - 1)
     wait_edges(0)
-    wait_rows(0, 0)
+    wait_rows(0, 0, 0)
 
     def greet(r):
         for n in (2**r, ring - 2**r):
@@ -277,7 +286,11 @@
     def step(c, _):
         @pl.when(c + AHEAD < tiles)
         def _():
-            start_tile(c + AHEAD)
+            start_tile(0, c + AHEAD)
+
+        @pl.when(c + AHEAD - 1 < tiles)
+        def _():
+            start_tile(1, c + AHEAD - 1)
 
         for r in range(rounds):
 
@@ -295,11 +308,12 @@
         def _():
             wait_edges(1)
 
-        wait_tile(c)
+        wait_tile(0, c)
         start_z(z_at(c), c)
 
         @pl.when(c == 1)
         def _():
+            wait_rows(1, 0, 0)
             wait_z(z_first, tiles)
             half(-1, inner, 7, 1)
             half(-1, outer, 7, 1)
@@ -311,6 +325,7 @@
 
         @pl.when(c >= 1)
         def _():
+            wait_tile(1, c - 1)
             half(c - 1, inner)
             wait_z(z_at(c - 1), c - 1)
             half(c - 1, outer)
@@ -341,10 +356,11 @@
         return 0
 
     lax.fori_loop(0, tiles, step, 0)
-    half(last, inner, 0, 7)
     wait_z(z_at(last), last)
+    wait_rows(1, 1, last)
     half(last, outer, 0, 7)
     start_h(h_last, last)
+    half(last, inner, 0, 7)
 
     @pl.when(has_edge(gx, 1))
     def _():
@@ -456,7 +472,9 @@
         to = {"gx": lax.rem(gx + d, nx)}
         at = pl.ds(8, rows)
         copy(E.at[1, :, at, :], E.at[1, :, at, :], xsE.at[d], xrE.at[0, d, 0], to).wait_send()
-        copy(F.at[:, 1, :, at, :], F.at[:, 1, :, at, :], xsF.at[d], xrF.at[0, d, 0], to).wait_send()
+        copy(E.at[1, :, at, :], E.at[1, :, at, :], xsK.at[d], xrK.at[0, d, 0], to).wait_send()
+        three = F.at[pl.ds(0, 3), 1, :, at, :]
+        copy(three, three, xsU.at[d], xrU.at[0, d, 0], to).wait_send()
         for side in (0, 1):
 
             @pl.when(has_edge(lax.rem(gx + d, nx), side))
@@ -501,7 +519,7 @@
             pltpu.VMEM((32, 1, 128), f32),
             pltpu.VMEM((8, 1, 128), f32),
             pltpu.VMEM((2, 1, 128), f32),
-            dma((4,)), dma((4,)), dma((2, 4, 8)), dma((2, 4, 8)),
+            dma((4,)), dma((4,)), dma((4,)), dma((2, 4, 8)), dma((2, 4, 8)), dma((2, 4, 8)),
             dma((4, 2)), dma((4, 2)), dma((4, 2)), dma((4, 2)), dma((2,)), dma((2,)),
             dma((2,)), dma((2,)), dma((2,)), dma((2, 9)), dma((2, 9)), dma((2, 9)),
             dma((8,)), dma((8,)),

time: 89.2 us -> 86.1 us (0.965)
  Pallas kernels: 86.5 us -> 83.8 us
    pallas_call x1, Pallas kernels: 86.5 us -> 83.8 us  [per_device(): pl.pallas_call(functools.partial(kernel, nx, ny, nz), out_shape=(jax.Shap...]
where the time goes in v6:
time: 86.1 us; the launch traced here: 85.9 us
  Pallas kernels  83.8 us (97%)
  local copies, waits for them, and re-layouts  1.49 us (2%)
    pallas_call x1, Pallas kernels, per_device(): pl.pallas_call(functools.partial(kernel, nx, ny, nz), out_shape=(jax.Shap...  83.8 us

profile of v6, /device:TPU:24, one launch (start us, length us, event | category | flops | bytes accessed | tf_op | source)
XLA Modules:
  0.0 85.9 jit_solution(17025429102429614092)
XLA Ops:
  0.6 83.8 %two_steps.1 = (f32[32,64,128]{2,1,0:T(8,128)S(1)}, f32[8,128]{1,0:T(8,128)S(1)}, f32[8,128]{1,0:T(8,128)S(1)}) custom-call(f32[32,8,8,128]{3,2,1,0:T(8,128)} %bitcast.11, f32[4,32,8,8,128]{4,3,2,1,0:T(8,128)} %bitcast.10), custom_call_target="tpu_custom_call" | custom-call | tf_op jit(solution)/shard_map/two_steps/pallas_call | solution.py:504
  84.5 0.5 slice_bitcast_fusion
  85.0 1.0 %copy.6 = f32[32,64,128]{2,1,0:T(8,128)} copy(f32[32,64,128]{2,1,0:T(8,128)S(1)} %get-tuple-element.14) | data formatting | bytes 2097152

commit v7 on v6

--- a/solution.py
+++ b/solution.py
@@ -54,7 +54,7 @@
 
 
 def kernel(
-    nx, ny, nz, e_ref, f_ref, o_ref, pm_ref, rm_ref, E, F, H, N, acc, SA, SC, SM,
+    nx, ny, nz, e_ref, f_ref, o_ref, pm_ref, rm_ref, E, F, H, N, below_row, acc, SA, SC, SM,
     xsE, xsK, xsU, xrE, xrK, xrU, gsE, gsK, grE, grK, xsH, xrH, zsE, zsK, zsH, zrE, zrK, zrH,
     osem, orem, sa_s, sa_r, sc_s, sc_r, tok,
 ):
@@ -115,9 +115,9 @@
         return [copy(a, b, s.at[d, side], r.at[d, side], {"gx": t}) for a, b, s, r in parts]
 
     def x_half(side):
-        src, dst = ((7, 71), (70, 6))[side]
+        src = H.at[pl.ds(1, 4), :, pl.ds((7, 70)[side], 1), :]
         return copy(
-            H.at[pl.ds(1, 4), :, pl.ds(src, 1), :], H.at[pl.ds(1, 4), :, pl.ds(dst, 1), :],
+            src, below_row if side else H.at[pl.ds(1, 4), :, pl.ds(71, 1), :],
             xsH.at[side], xrH.at[side], {"gx": lax.rem(gx + (nx - 1, 1)[side], nx)},
         )
 
@@ -194,10 +194,15 @@
 
         over(planes, plane)
 
-    def full(c, planes):
+    def full(c, planes, first=0, count=8):
         def plane(p):
             v = change_of(H, p, 8 * c + 7, F, pl.multiple_of(8 * c + 8, 8))
-            N[p - 1, :, pl.ds(pl.multiple_of(8 * c, 8), 8), :] = v
+            if count < 8:
+                N[p - 1, :, pl.ds(8 * c + first, count), :] = v[:, first : first + count]
+                row = lax.broadcasted_iota(jnp.int32, v.shape, 1)
+                v = jnp.where((row >= first) & (row < first + count), v, 0.0)
+            else:
+                N[p - 1, :, pl.ds(pl.multiple_of(8 * c, 8), 8), :] = v
             acc[p - 1] += jnp.sum(v, axis=0)
 
         over(planes, plane)
@@ -333,11 +338,10 @@
 
         @pl.when(c == 2)
         def _():
+            full(0, inner, 1, 7)
             wait_h(h_first, tiles)
-
-        @pl.when(c == 2)
-        def _():
             wait_h(h_at(0), 0)
+            full(0, outer, 1, 7)
 
         @pl.when(c >= 3)
         def _():
@@ -347,6 +351,7 @@
 
         @pl.when(c == 4)
         def _():
+            send_out(pl.ds(1, 7))
             send_out(out_at(1))
 
         @pl.when(c >= 4)
@@ -369,7 +374,6 @@
     full(last - 1, inner)
     wait_h(h_at(last - 1), last - 1)
     full(last - 1, outer)
-    send_out(out_at(last - 1))
 
     @pl.when(has_edge(gx, 1))
     def _():
@@ -382,9 +386,10 @@
     @pl.when(has_edge(gx, 0))
     def _():
         x_half(1).wait_recv()
-
-    full(0, inner)
-    full(0, outer)
+        H[1:5, :, 6:7, :] = below_row[...]
+
+    full(0, inner, 0, 1)
+    full(0, outer, 0, 1)
 
     lane = lax.broadcasted_iota(jnp.int32, (1, 128), 1)
     part = jnp.zeros((1, 128), jnp.float32)
@@ -411,8 +416,9 @@
         return 0
 
     lax.fori_loop(1, nx * ny, start_row, 0)
+    send_out(out_at(last - 1))
     send_out(out_at(last))
-    send_out(out_at(0))
+    send_out(pl.ds(0, 1))
     lax.fori_loop(1, nx * ny, wait_row, 0)
     planes = jnp.sum(SA[...], axis=0)
     SM[1] = planes
@@ -515,6 +521,7 @@
             pltpu.VMEM((4, 6, 8, 80, 128), f32),
             pltpu.VMEM((6, 8, 80, 128), f32),
             pltpu.VMEM((4, 8, 64, 128), f32),
+            pltpu.VMEM((4, 8, 1, 128), f32),
             pltpu.VMEM((4, 8, 128), f32),
             pltpu.VMEM((32, 1, 128), f32),
             pltpu.VMEM((8, 1, 128), f32),

time: 86.1 us -> 85.1 us (0.988)
  Pallas kernels: 83.8 us -> 82.8 us
    pallas_call x1, Pallas kernels: 83.8 us -> 82.8 us  [per_device(): pl.pallas_call(functools.partial(kernel, nx, ny, nz), out_shape=(jax.Shap...]
where the time goes in v7:
time: 85.1 us; the launch traced here: 85 us
  Pallas kernels  82.8 us (97%)
  local copies, waits for them, and re-layouts  1.49 us (2%)
    pallas_call x1, Pallas kernels, per_device(): pl.pallas_call(functools.partial(kernel, nx, ny, nz), out_shape=(jax.Shap...  82.8 us

profile of v7, /device:TPU:24, one launch (start us, length us, event | category | flops | bytes accessed | tf_op | source)
XLA Modules:
  0.0 85.0 jit_solution(14580165148430340314)
XLA Ops:
  0.6 82.8 %two_steps.1 = (f32[32,64,128]{2,1,0:T(8,128)S(1)}, f32[8,128]{1,0:T(8,128)S(1)}, f32[8,128]{1,0:T(8,128)S(1)}) custom-call(f32[32,8,8,128]{3,2,1,0:T(8,128)} %bitcast.11, f32[4,32,8,8,128]{4,3,2,1,0:T(8,128)} %bitcast.10), custom_call_target="tpu_custom_call" | custom-call | tf_op jit(solution)/shard_map/two_steps/pallas_call | solution.py:510
  83.5 0.5 slice_bitcast_fusion
  84.0 1.0 %copy.6 = f32[32,64,128]{2,1,0:T(8,128)} copy(f32[32,64,128]{2,1,0:T(8,128)S(1)} %get-tuple-element.14) | data formatting | bytes 2097152

commit v8 on v7

--- a/solution.py
+++ b/solution.py
@@ -54,9 +54,9 @@
 
 
 def kernel(
-    nx, ny, nz, e_ref, f_ref, o_ref, pm_ref, rm_ref, E, F, H, N, below_row, acc, SA, SC, SM,
+    nx, ny, nz, e_ref, f_ref, o_ref, pm_ref, rm_ref, E, F, H, N, below_row, first_tile, acc, SA, SC, SM,
     xsE, xsK, xsU, xrE, xrK, xrU, gsE, gsK, grE, grK, xsH, xrH, zsE, zsK, zsH, zrE, zrK, zrH,
-    osem, orem, sa_s, sa_r, sc_s, sc_r, tok,
+    osem, orem, fsem, sa_s, sa_r, sc_s, sc_r, tok,
 ):
     gx, gy, gz = (lax.axis_index(a) for a in ("gx", "gy", "gz"))
     ring = ny * nz
@@ -81,13 +81,15 @@
             device_id_type=MESH,
         )
 
-    def x_rows(kind, d, part, c):
+    def x_rows(kind, d, part, c, staged=False):
         t = lax.rem(gx + d, nx)
         inside = (pl.ds(0, 2), pl.ds(2, 6))[part]
         at = pl.ds(8 + 8 * c + 2 * part, (2, 6)[part])
+        e_from = first_tile.at[0, t] if staged else e_ref.at[t * tiles + c]
+        k_from = first_tile.at[1, t] if staged else f_ref.at[3, t * tiles + c]
         parts = (
-            (e_ref.at[t * tiles + c, :, inside, :], E.at[1 + gx, :, at, :], xsE, xrE),
-            (f_ref.at[3, t * tiles + c, :, inside, :], F.at[3, 1 + gx, :, at, :], xsK, xrK),
+            (e_from.at[:, inside, :], E.at[1 + gx, :, at, :], xsE, xrE),
+            (k_from.at[:, inside, :], F.at[3, 1 + gx, :, at, :], xsK, xrK),
             (
                 f_ref.at[pl.ds(0, 3), t * tiles + c, :, inside, :],
                 F.at[pl.ds(0, 3), 1 + gx, :, at, :],
@@ -124,9 +126,9 @@
     def has_edge(g, side):
         return g > 0 if side == 0 else g < nx - 1
 
-    def start_rows(kind, part, c):
+    def start_rows(kind, part, c, staged=False):
         for d in range(nx):
-            for x in x_rows(kind, d, part, c):
+            for x in x_rows(kind, d, part, c, staged and d > 0):
                 x.start()
 
     def start_tile(kind, c):
@@ -229,6 +231,16 @@
     def out_at(c):
         return pl.ds(pl.multiple_of(8 * c, 8), 8)
 
+    def stage(d):
+        t = lax.rem(gx + d, nx)
+        return (
+            pltpu.make_async_copy(e_ref.at[t * tiles], first_tile.at[0, t], fsem.at[0, d]),
+            pltpu.make_async_copy(f_ref.at[3, t * tiles], first_tile.at[1, t], fsem.at[1, d]),
+        )
+
+    for d in range(1, nx):
+        for x in stage(d):
+            x.start()
     acc[...] = jnp.zeros_like(acc)
     for side, at, half_at in ((0, 7, 6), (1, 8 + rows, 7 + rows)):
 
@@ -240,9 +252,13 @@
             H[1:5, :, half_at : half_at + 1, :] = none
 
     pl.semaphore_wait(bar, nx + 1)
+    for d in range(1, nx):
+        for x in stage(d):
+            x.wait()
+    start_rows(0, 1, 0, True)
+    start_rows(0, 0, 0, True)
+    start_rows(0, 0, 1)
     start_edges(0)
-    start_rows(0, 0, 0)
-    start_tile(0, 0)
     start_edges(1)
     start_rows(1, 0, 0)
     for c in range(1, AHEAD):
@@ -522,6 +538,7 @@
             pltpu.VMEM((6, 8, 80, 128), f32),
             pltpu.VMEM((4, 8, 64, 128), f32),
             pltpu.VMEM((4, 8, 1, 128), f32),
+            pltpu.VMEM((2, 4, 8, 8, 128), f32),
             pltpu.VMEM((4, 8, 128), f32),
             pltpu.VMEM((32, 1, 128), f32),
             pltpu.VMEM((8, 1, 128), f32),
@@ -529,7 +546,7 @@
             dma((4,)), dma((4,)), dma((4,)), dma((2, 4, 8)), dma((2, 4, 8)), dma((2, 4, 8)),
             dma((4, 2)), dma((4, 2)), dma((4, 2)), dma((4, 2)), dma((2,)), dma((2,)),
             dma((2,)), dma((2,)), dma((2,)), dma((2, 9)), dma((2, 9)), dma((2, 9)),
-            dma((8,)), dma((8,)),
+            dma((8,)), dma((8,)), dma((2, 4)),
             dma((32,)), dma((32,)), dma((8, 4)), dma((8,)),
             pltpu.SemaphoreType.REGULAR((8,)),
         ],

time: 85.1 us -> 85 us (level)
  no operation moved by 1% of the time
where the time goes in v8:
time: 85 us; the launch traced here: 84.8 us
  Pallas kernels  82.7 us (97%)
  local copies, waits for them, and re-layouts  1.49 us (2%)
    pallas_call x1, Pallas kernels, per_device(): pl.pallas_call(functools.partial(kernel, nx, ny, nz), out_shape=(jax.Shap...  82.7 us

profile of v8, /device:TPU:24, one launch (start us, length us, event | category | flops | bytes accessed | tf_op | source)
XLA Modules:
  0.0 84.8 jit_solution(8619256094095175888)
XLA Ops:
  0.6 82.7 %two_steps.1 = (f32[32,64,128]{2,1,0:T(8,128)S(1)}, f32[8,128]{1,0:T(8,128)S(1)}, f32[8,128]{1,0:T(8,128)S(1)}) custom-call(f32[32,8,8,128]{3,2,1,0:T(8,128)} %bitcast.11, f32[4,32,8,8,128]{4,3,2,1,0:T(8,128)} %bitcast.10), custom_call_target="tpu_custom_call" | custom-call | tf_op jit(solution)/shard_map/two_steps/pallas_call | solution.py:526
  83.3 0.5 slice_bitcast_fusion
  83.9 1.0 %copy.6 = f32[32,64,128]{2,1,0:T(8,128)} copy(f32[32,64,128]{2,1,0:T(8,128)S(1)} %get-tuple-element.14) | data formatting | bytes 2097152
